TPU v7x, 32 devices: a whole 2x2x4 slice. The times are simulated.
32 devices in a mesh: face: 2 (over core), tile: 16 (over z, y, x).
Axes of the slice: x: 2, y: 2, z: 4, core: 2. Of those that a mesh axis runs over, the one named last changes fastest.
Arguments:
- crm_state: bfloat16 [6, 72, 32768], P(None, None, ('face', 'tile')), may hold values from -4 to 4
- active_levels: int32 [1024], P(('face', 'tile')), may hold values from 18 to 72
- mix_x: float32 [1024], P(('face', 'tile')), may hold values from 0.05 to 0.2
- drift_speed: float32 [1024], P(('face', 'tile')), may hold values from -0.1 to 0.1
- cond_rate: float32 [1024], P(('face', 'tile')), may hold values from 0.2 to 0.8
- mix_z: float32 [72], replicated, may hold values from 0.02 to 0.2
- point_mass: float32 [4096], P(('face', 'tile')), may hold values from 0.3 to 3
- neighbor_slots: int32 [4, 256], P(None, ('face', 'tile')), may hold values from 0 to 39, as said below
- edge_codes: int32 [4, 256], P(None, ('face', 'tile')), may hold values from 0 to 7, as said below
Outputs:
- new_state: bfloat16 [6, 72, 32768], P(None, None, ('face', 'tile'))
- gll_tendency: float32 [6, 72, 4096], P(None, None, ('face', 'tile'))
Inputs may be any that keep to these rules, and one draw needn't show every extreme that they name: `neighbor_slots`: v // 8 is 0 for this device, 1 for tile index - 1, 2 for tile index + 1, 3 for face index - 1, 4 for face index + 1 (indices wrapping), and v % 8 the element there. The relation is mutual: if e names b across one of its edges, b names e across one of its own. On every device exactly 4 elements name an element on tile index - 1, 4 on tile index + 1, 2 on face index - 1 and 2 on face index + 1, each exactly one such element. `edge_codes`: 2 k' + r: k' is the neighbour's own edge that is shared, and r is 1 when the two elements list that edge's cells and points in opposite senses. Codes agree from both sides of every edge.
All inputs are finite; a program needn't handle non-finite values.
Results may differ from a plain program's by a relative error of at most 0.001.
Values sent between devices are 32-bit elements; how exact they have to be, the bound alone decides.
No kernel may reach another device: no remote copies, remote signals or barrier semaphores. Data moves between devices by JAX's collectives and lax.ppermute only.
A program may use at most 64 MiB of HBM per device.

v0:
```python
import math

import jax
import jax.numpy as jnp
import numpy as np
from jax import lax
from jax.sharding import PartitionSpec as P

NSUB = 2
BLK_R = 4
BLK_C = 2


per_time = 10.0
CELL_EDGE = [[0, 1], [1, 3], [2, 3], [0, 2]]
GLL_EDGE = [[0, 1, 2, 3], [3, 7, 11, 15], [12, 13, 14, 15], [0, 4, 8, 12]]


def passed_along(value, axis, steps):
    count = lax.axis_size(axis)
    pairs = [(source, (source + steps) % count) for source in range(count)]
    return lax.ppermute(value, axis, pairs)


def oriented(edge_lists):
    row_list = []
    for edge_code in range(8):
        edge_side = list(edge_lists[edge_code // 2])
        if edge_code % 2 == 1:
            edge_side = edge_side[::-1]
        row_list.append(edge_side)
    return np.array(row_list, np.int32)


def lagrange(q, z):
    centres = [-1.5, -0.5, 0.5, 1.5]
    product = 1.0
    for r in range(4):
        if r != q:
            product = product * (z - centres[r]) / (centres[q] - centres[r])
    return product


def linear_weight(j, z):
    return 0.5 - z if j == 0 else 0.5 + z


def remap_matrix():
    gll_nodes = [-1.0, -1.0 / math.sqrt(5.0), 1.0 / math.sqrt(5.0), 1.0]
    matrix = [[0.0 for column in range(12)] for row in range(16)]
    for b in range(4):
        for a in range(4):
            p = 4 * b + a
            x = gll_nodes[a]
            y = gll_nodes[b]
            for j in range(2):
                for i in range(2):
                    matrix[p][2 * j + i] += 0.5 * linear_weight(j, y) * lagrange(
                        1 + i, x
                    ) + 0.5 * linear_weight(i, x) * lagrange(1 + j, y)
            for m in range(2):
                matrix[p][4 + 6 + m] += 0.5 * linear_weight(m, y) * lagrange(0, x)
                matrix[p][4 + 2 + m] += 0.5 * linear_weight(m, y) * lagrange(3, x)
                matrix[p][4 + 0 + m] += 0.5 * linear_weight(m, x) * lagrange(0, y)
                matrix[p][4 + 4 + m] += 0.5 * linear_weight(m, x) * lagrange(3, y)
    return np.array(matrix, np.float32)


def select_codes(code_values, code_table):
    compare = code_values[..., None] == jnp.arange(8, dtype=jnp.int32)
    return jnp.sum(
        jnp.where(compare[..., None], jnp.asarray(code_table)[None, None, :, :], 0), axis=2
    ).astype(jnp.int32)


def microphysics(prognostic_bundle, alive_indicator, cond_speed):
    thermal_profile = prognostic_bundle[0]
    gaseous_moisture = prognostic_bundle[1]
    cloud_droplets = prognostic_bundle[2]
    icy_hydrometeor = prognostic_bundle[3]
    humidity_ceiling = 0.5 * jnp.exp(0.3 * thermal_profile)
    droplet_growth_increment = jnp.where(
        alive_indicator,
        jnp.maximum(cond_speed * (gaseous_moisture - humidity_ceiling), -cloud_droplets),
        0.0,
    )
    gaseous_moisture = gaseous_moisture - droplet_growth_increment
    cloud_droplets = cloud_droplets + droplet_growth_increment
    thermal_profile = thermal_profile + 0.5 * droplet_growth_increment
    glaciation_increment = jnp.where(
        alive_indicator, 0.3 * cloud_droplets * jax.nn.sigmoid(-2.0 * thermal_profile), 0.0
    )
    cloud_droplets = cloud_droplets - glaciation_increment
    icy_hydrometeor = icy_hydrometeor + glaciation_increment
    thermal_profile = thermal_profile + 0.1 * glaciation_increment
    return jnp.stack(
        [
            thermal_profile,
            gaseous_moisture,
            cloud_droplets,
            icy_hydrometeor,
            prognostic_bundle[4],
            prognostic_bundle[5],
        ]
    )


def cell_shift_tile(members, step_by):
    return (passed_along(members[0], "tile", step_by),)


def cell_shift_face(members, step_by):
    return (passed_along(members[0], "face", step_by),)


def point_shift_tile(members, step_by):
    return passed_along((members[0], members[1]), "tile", step_by)


def point_shift_face(members, step_by):
    return passed_along((members[0], members[1]), "face", step_by)


def collect(members, neighbor_slots, shift_tile, shift_face):
    element_count = neighbor_slots.shape[1]
    serial = jnp.arange(element_count, dtype=jnp.int32)
    pieces = [members]
    lookup_parts = [serial]
    offset = element_count
    directions = (
        (1, shift_tile, 1, 2, BLK_R),
        (2, shift_tile, -1, 1, BLK_R),
        (3, shift_face, 1, 4, BLK_C),
        (4, shift_face, -1, 3, BLK_C),
    )
    for incoming, sender, step_by, outgoing, boundary in directions:
        lookup_parts.append(offset + serial)
        offset = offset + element_count
        pieces.append(sender(members, step_by))
    merged = tuple(
        (jnp.concatenate([piece[n] for piece in pieces], axis=0) for n in range(len(members)))
    )
    lookup = jnp.concatenate(lookup_parts)
    pool_rows = jnp.take(lookup, neighbor_slots)
    return (merged, pool_rows)


def local(
    crm_state,
    active_levels,
    mix_x,
    drift_speed,
    cond_rate,
    mix_z,
    point_mass,
    neighbor_slots,
    edge_codes,
):
    element_count = neighbor_slots.shape[1]
    fields_count = crm_state.shape[0]
    levels = crm_state.shape[1]
    columns = active_levels.shape[0]
    width = crm_state.shape[2] // columns
    flat_len = fields_count * levels
    initial = crm_state.astype(jnp.float32)
    position_x = jnp.arange(columns * width, dtype=jnp.int32) % width
    at_last = position_x == width - 1
    at_first = position_x == 0
    alive_indicator = (
        jnp.arange(levels, dtype=jnp.int32)[:, None] < jnp.repeat(active_levels, width)[None, :]
    )
    coupling = jnp.where(jnp.arange(levels, dtype=jnp.int32) < levels - 1, mix_z, 0.0)[:, None]
    mix_horiz = jnp.repeat(mix_x, width)
    shift_rate = jnp.repeat(drift_speed, width)
    cond_speed = jnp.repeat(cond_rate, width)
    current = initial
    for substep in range(NSUB):
        east_side = jnp.where(
            at_last, jnp.roll(current, width - 1, axis=2), jnp.roll(current, -1, axis=2)
        )
        west_side = jnp.where(
            at_first, jnp.roll(current, 1 - width, axis=2), jnp.roll(current, 1, axis=2)
        )
        current = (
            current
            + mix_horiz * (east_side - 2.0 * current + west_side)
            + 0.5 * shift_rate * (west_side - east_side)
        )
        level_above = jnp.concatenate([current[:, 1:], current[:, -1:]], axis=1)
        flux_up = coupling * (level_above - current)
        flux_below = jnp.concatenate([jnp.zeros_like(flux_up[:, :1]), flux_up[:, :-1]], axis=1)
        current = current + flux_up - flux_below
        current = microphysics(current, alive_indicator, cond_speed)
    new_state = current.astype(jnp.bfloat16)
    tendency = (
        jnp.mean((current - initial).reshape(fields_count, levels, columns, width), axis=3)
        * per_time
    )
    cell_values = tendency.reshape(flat_len, element_count, 4).transpose(1, 2, 0)
    matrix = jnp.asarray(remap_matrix(), jnp.float32)
    masses = point_mass.reshape(element_count, 16)
    point_pick = select_codes(edge_codes, oriented(GLL_EDGE))
    cell_pools, cell_rows = collect(
        (cell_values,), neighbor_slots, cell_shift_tile, cell_shift_face
    )
    cell_pick = select_codes(edge_codes, oriented(CELL_EDGE))
    gather_index = (cell_rows[:, :, None] * 4 + cell_pick).transpose(1, 0, 2).reshape(-1)
    flat_cells = cell_pools[0].reshape(-1, flat_len)
    neighbours = jnp.take(flat_cells, gather_index, axis=0).reshape(element_count, 8, flat_len)
    stacked = jnp.concatenate([cell_values, neighbours], axis=1)
    points = jnp.einsum("ecz,pc->epz", stacked, matrix, precision=lax.Precision.HIGHEST)
    point_pools, point_rows = collect(
        (points, masses), neighbor_slots, point_shift_tile, point_shift_face
    )
    flat_weighted = (point_pools[0] * point_pools[1][:, :, None]).reshape(-1, flat_len)
    flat_mass = point_pools[1].reshape(-1)
    numerator = points * masses[:, :, None]
    denominator = masses
    for k in range(4):
        point_index = (point_rows[k][:, None] * 16 + point_pick[k]).reshape(-1)
        numerator = numerator.at[:, GLL_EDGE[k]].add(
            jnp.take(flat_weighted, point_index, axis=0).reshape(element_count, 4, flat_len)
        )
        denominator = denominator.at[:, GLL_EDGE[k]].add(
            jnp.take(flat_mass, point_index).reshape(element_count, 4)
        )
    ratio = numerator / denominator[:, :, None]
    gll_tendency = ratio.transpose(2, 0, 1).reshape(fields_count, levels, 16 * element_count)
    return (new_state, gll_tendency)


def solution(mesh):
    in_specs = (
        P(None, None, ("face", "tile")),
        P(("face", "tile")),
        P(("face", "tile")),
        P(("face", "tile")),
        P(("face", "tile")),
        P(),
        P(("face", "tile")),
        P(None, ("face", "tile")),
        P(None, ("face", "tile")),
    )
    out_specs = (P(None, None, ("face", "tile")), P(None, None, ("face", "tile")))
    return jax.shard_map(local, mesh=mesh, in_specs=in_specs, out_specs=out_specs, check_vma=False)
```

profile of v0, /device:TPU:0, one launch (start us, length us, event | category | flops | bytes accessed | tf_op | source)
XLA Modules:
  0.0 81.0 jit_solution(4142714394118590489)
XLA Ops:
  0.6 1.8 %copy.76 = bf16[6,72,1024]{1,2,0:T(8,128)(2,1)S(1)} copy(bf16[6,72,1024]{2,1,0:T(8,128)(2,1)} %param.26) | data formatting | bytes 1769472 | tf_op args[0]
  2.4 3.0 %fusion.20 = (f32[6,72,1023]{1,2,0:T(8,128)}, f32[6,72,1023]{1,2,0:T(8,128)}) fusion(bf16[6,72,1024]{1,2,0:T(8,128)(2,1)S(1)} %copy.76), kind=kLoop, calls=%fused_computation.139 | loop fusion | bytes 7070976 | tf_op jit(solution)/shard_map/jit(_roll_static)/slice | solution.py:179
  5.4 3.0 %fusion.19 = (f32[6,72,993]{1,2,0:T(8,128)}, f32[6,72,993]{1,2,0:T(8,128)}) fusion(bf16[6,72,1024]{1,2,0:T(8,128)(2,1)S(1)} %copy.76), kind=kLoop, calls=%fused_computation.138 | loop fusion | bytes 6863616 | tf_op jit(solution)/shard_map/jit(_roll_static)/slice | solution.py:179
  8.8 7.4 %multiply_add_fusion.1 = f32[6,72,1024]{1,2,0:T(8,128)S(1)} fusion(f32[6,72,1023]{1,2,0:T(8,128)} %get-tuple-element.40, f32[6,72,1]{1,2,0:T(1,128)S(1)} %get-tuple-element.42, f32[6,72,31]{1,2,0:T(8,128)S(1)} %get-tuple-element.36, f32[6,72,993]{1,2,0:T(8,128)} %get-tuple-element.38, f32[6,72,1]{1,2,0:T(1,128)S(1)} %get-tuple-element.41, ...), kind=kLoop, calls=%fused_computation.30 | loop fusion | flops 6635520 | bytes 9742336 | tf_op jit(solution)/shard_map/add | solution.py:185
  16.2 0.9 %slice.200 = f32[6,71,1024]{1,2,0:T(8,128)S(1)} slice(f32[6,72,1024]{1,2,0:T(8,128)S(1)} %multiply_add_fusion.1), slice={[0:6], [1:72], [0:1024]} | slice | bytes 3489792 | tf_op jit(solution)/shard_map/slice | solution.py:189
  17.1 0.9 %slice.201 = f32[6,1,1024]{1,2,0:T(8,128)S(1)} slice(f32[6,72,1024]{1,2,0:T(8,128)S(1)} %multiply_add_fusion.1), slice={[0:6], [71:72], [0:1024]} | slice | bytes 49152 | tf_op jit(solution)/shard_map/slice | solution.py:189
  17.9 0.9 %fusion = f32[6,72,1024]{1,2,0:T(8,128)S(1)} fusion(f32[6,72,1024]{1,2,0:T(8,128)S(1)} %multiply_add_fusion.1, f32[6,1,1024]{1,2,0:T(8,128)S(1)} %slice.201, f32[6,71,1024]{1,2,0:T(8,128)S(1)} %slice.200, f32[72]{0:T(128)S(1)} %compare_select_fusion.8), kind=kLoop, calls=%fused_computation.21 | loop fusion | flops 1327104 | bytes 5308704 | tf_op jit(solution)/shard_map/mul | solution.py:190
  18.9 2.5 %pad_subtract_fusion.1 = f32[6,72,1024]{1,2,0:T(8,128)} fusion(f32[6,71,1024]{1,2,0:T(8,128)S(1)} %bitcast.52, f32[6,72,1024]{1,2,0:T(8,128)S(1)} %multiply_add_fusion.1, f32[6,72,1024]{1,2,0:T(8,128)S(1)} %fusion), kind=kLoop, calls=%fused_computation.29 | loop fusion | flops 884736 | bytes 7053312 | tf_op jit(solution)/shard_map/sub | solution.py:192
  21.7 2.0 %add_dynamic-update-slice_fusion.1 = (f32[6,72,1024]{1,2,0:T(8,128)S(1)}, f32[1,72,1024]{1,2,0:T(8,128)S(1)}, f32[1,72,1024]{1,2,0:T(8,128)S(1)}) fusion(f32[6,72,1024]{1,2,0:T(8,128)} %pad_subtract_fusion.1, s32[1024]{0:T(1024)S(1)} %lt.115, f32[1024]{0:T(1024)S(1)} %mul.262), kind=kLoop, calls=%fused_computation.48 | loop fusion | flops 1474559 | bytes 2465792
  25.3 4.8 %multiply_add_fusion = f32[6,72,1024]{1,2,0:T(8,128)S(1)} fusion(f32[6,72,1024]{1,2,0:T(8,128)S(1)} %slice_dynamic-update-slice_fusion.1, f32[6,72,1023]{1,2,0:T(8,128)S(1)} %get-tuple-element.32, f32[6,72,1]{1,2,0:T(1,128)S(1)} %get-tuple-element.34, f32[6,72,31]{1,2,0:T(8,128)S(1)} %get-tuple-element.28, f32[6,72,993]{1,2,0:T(8,128)S(1)} %get-tuple-element.30, ...), kind=kLoop, calls=%fused_computation.28 | loop fusion | flops 6193152 | bytes 10627072 | tf_op jit(solution)/shard_map/add | solution.py:185
  30.1 0.9 %slice.216 = f32[6,71,1024]{1,2,0:T(8,128)S(1)} slice(f32[6,72,1024]{1,2,0:T(8,128)S(1)} %multiply_add_fusion), slice={[0:6], [1:72], [0:1024]} | slice | bytes 3489792 | tf_op jit(solution)/shard_map/slice | solution.py:189
  30.9 0.9 %slice.217 = f32[6,1,1024]{1,2,0:T(8,128)S(1)} slice(f32[6,72,1024]{1,2,0:T(8,128)S(1)} %multiply_add_fusion), slice={[0:6], [71:72], [0:1024]} | slice | bytes 49152 | tf_op jit(solution)/shard_map/slice | solution.py:189
  31.8 0.9 %fusion.1 = f32[6,72,1024]{1,2,0:T(8,128)S(1)} fusion(f32[6,72,1024]{1,2,0:T(8,128)S(1)} %multiply_add_fusion, f32[6,1,1024]{1,2,0:T(8,128)S(1)} %slice.217, f32[6,71,1024]{1,2,0:T(8,128)S(1)} %slice.216, f32[72]{0:T(128)S(1)} %compare_select_fusion.8), kind=kLoop, calls=%fused_computation.25 | loop fusion | flops 1327104 | bytes 5308704 | tf_op jit(solution)/shard_map/mul | solution.py:190
  32.7 0.9 %pad_subtract_fusion = f32[6,72,1024]{1,2,0:T(8,128)S(1)} fusion(f32[6,71,1024]{1,2,0:T(8,128)S(1)} %bitcast.51, f32[6,72,1024]{1,2,0:T(8,128)S(1)} %multiply_add_fusion, f32[6,72,1024]{1,2,0:T(8,128)S(1)} %fusion.1), kind=kLoop, calls=%fused_computation.27 | loop fusion | flops 884736 | bytes 7053312 | tf_op jit(solution)/shard_map/sub | solution.py:192
  34.6 0.9 %bitcast_reduce_fusion = f32[6,72,32]{1,2,0:T(8,128)S(1)} fusion(f32[6,72,1024]{1,2,0:T(8,128)S(1)} %slice_dynamic-update-slice_fusion, bf16[6,72,1024]{1,2,0:T(8,128)(2,1)S(1)} %copy.76), kind=kLoop, calls=%fused_computation.26 | loop fusion | flops 1313280 | bytes 2709504 | tf_op jit(solution)/shard_map/reduce_sum | solution.py:196
  36.3 3.0 %collective-permute-start = (f32[8,4,432]{2,1,0:T(4,128)S(1)}, f32[8,4,432]{2,1,0:T(4,128)S(1)}, u32[]{:S(2)}, u32[]{:S(2)}) collective-permute-start(f32[8,4,432]{2,1,0:T(4,128)S(1)} %bitcast.53), channel_id=1, source_target_pairs={{0,1},{1,2},{2,3},{3,4},{4,5},{5,6},{6,7},{7,8},{8,9},{9,10},{10,1... | collective-permute-start | bytes 165896 | tf_op jit(solution)/shard_map/ppermute | solution.py:22
  39.3 4.1 %collective-permute-start.1 = (f32[8,4,432]{2,1,0:T(4,128)S(1)}, f32[8,4,432]{2,1,0:T(4,128)S(1)}, u32[]{:S(2)}, u32[]{:S(2)}) collective-permute-start(f32[8,4,432]{2,1,0:T(4,128)S(1)} %bitcast.54), channel_id=1, source_target_pairs={{0,15},{1,0},{2,1},{3,2},{4,3},{5,4},{6,5},{7,6},{8,7},{9,8},{10,9... | collective-permute-start | bytes 165896 | tf_op jit(solution)/shard_map/ppermute | solution.py:22
  43.5 5.6 %collective-permute-start.7 = (f32[8,16]{1,0:T(8,128)S(1)}, f32[8,16]{1,0:T(8,128)S(1)}, u32[]{:S(2)}, u32[]{:S(2)}) collective-permute-start(f32[8,16]{1,0:T(8,128)S(1)} %mul.289), channel_id=1, source_target_pairs={{0,15},{1,0},{2,1},{3,2},{4,3},{5,4},{6,5},{7,6},{8,7},{9,8},{10,9... | collective-permute-start | bytes 1544 | tf_op jit(solution)/shard_map/ppermute | solution.py:22
  52.6 2.1 %convert_element_type.7 = bf16[6,72,1024]{1,2,0:T(8,128)(2,1)S(1)} convert(f32[6,72,1024]{1,2,0:T(8,128)} %copy-done.1) | non-fusion elementwise | flops 442368 | bytes 2654208 | tf_op jit(solution)/shard_map/convert_element_type | solution.py:194
  54.7 1.4 %copy.95 = bf16[6,72,1024]{2,1,0:T(8,128)(2,1)} copy(bf16[6,72,1024]{1,2,0:T(8,128)(2,1)S(1)} %convert_element_type.7) | data formatting | bytes 1769472
  56.3 1.1 %collective-permute-done.8 = f32[8,16]{1,0:T(8,128)S(1)} collective-permute-done((f32[8,16]{1,0:T(8,128)S(1)}, f32[8,16]{1,0:T(8,128)S(1)}, u32[]{:S(2)}, u32[]{:S(2)}) %collective-permute-start.8) | collective-permute-done | bytes 544 | tf_op jit(solution)/shard_map/ppermute | solution.py:22
  61.7 5.6 %collective-permute-start.4 = (f32[8,16,432]{2,1,0:T(8,128)S(1)}, f32[8,16,432]{2,1,0:T(8,128)S(1)}, u32[]{:S(2)}, u32[]{:S(2)}) collective-permute-start(f32[8,16,432]{2,1,0:T(8,128)S(1)} %get-tuple-element.53), channel_id=1, source_target_pairs={{0,15},{1,0},{2,1},{3,2},{4,3},{5,4},{6,5},{7,6},{8,7},{9,8},{10,9... | collective-permute-start | bytes 663560 | tf_op jit(solution)/shard_map/ppermute | solution.py:22
  70.7 3.1 %collective-permute-done.3 = f32[8,16,432]{2,1,0:T(8,128)S(1)} collective-permute-done((f32[8,16,432]{2,1,0:T(8,128)S(1)}, f32[8,16,432]{2,1,0:T(8,128)S(1)}, u32[]{:S(2)}, u32[]{:S(2)}) %collective-permute-start.3) | collective-permute-done | bytes 221216 | tf_op jit(solution)/shard_map/ppermute | solution.py:22
  80.2 0.9 %copy.96 = f32[6,72,128]{2,1,0:T(8,128)} copy(f32[6,72,128]{1,0,2:T(8,128)S(1)} %reshape.335) | data formatting | bytes 442368
  (186 shorter events, 21.2 us)
Async XLA Ops:
  5.4 3.0 %copy-start.13 = (f32[32]{0:T(128)S(1)}, f32[32]{0:T(128)}, u32[]{:S(2)}) copy-start(f32[32]{0:T(128)} %param.29) | copy-start | bytes 388
  5.4 3.2 %copy-start.9 = (f32[32]{0:T(128)S(1)}, f32[32]{0:T(128)}, u32[]{:S(2)}) copy-start(f32[32]{0:T(128)} %param.28) | copy-start | bytes 388
  17.0 0.9 %copy-start.14 = (f32[72]{0:T(128)S(1)}, f32[72]{0:T(128)}, u32[]{:S(2)}) copy-start(f32[72]{0:T(128)} %param.31) | copy-start | bytes 868
  18.8 2.5 %copy-start.10 = (s32[32]{0:T(128)S(1)}, s32[32]{0:T(128)}, u32[]{:S(2)}) copy-start(s32[32]{0:T(128)} %param.27) | copy-start | bytes 388
  18.9 2.7 %copy-start.11 = (f32[32]{0:T(128)S(1)}, f32[32]{0:T(128)}, u32[]{:S(2)}) copy-start(f32[32]{0:T(128)} %param.30) | copy-start | bytes 388
  21.7 2.4 %copy-start = (f32[6,72,1024]{1,2,0:T(8,128)S(1)}, f32[6,72,1024]{1,2,0:T(8,128)}, u32[]{:S(2)}) copy-start(f32[6,72,1024]{1,2,0:T(8,128)} %pad_subtract_fusion.1) | copy-start | bytes 5308420
  34.5 1.6 %copy-start.1 = (f32[6,72,1024]{1,2,0:T(8,128)}, f32[6,72,1024]{1,2,0:T(8,128)S(1)}, u32[]{:S(2)}) copy-start(f32[6,72,1024]{1,2,0:T(8,128)S(1)} %slice_dynamic-update-slice_fusion) | copy-start | bytes 5308420
  34.5 8.9 %copy-start.12 = (f32[128]{0:T(128)S(1)}, f32[128]{0:T(128)}, u32[]{:S(2)}) copy-start(f32[128]{0:T(128)} %param.32) | copy-start | bytes 1540
  34.5 14.6 %copy-start.3 = (s32[4,8]{1,0:T(4,128)S(1)}, s32[4,8]{1,0:T(4,128)}, u32[]{:S(2)}) copy-start(s32[4,8]{1,0:T(4,128)} %param.33) | copy-start | bytes 388
  34.5 15.6 %copy-start.6 = (s32[4,8]{1,0:T(4,128)S(1)}, s32[4,8]{1,0:T(4,128)}, u32[]{:S(2)}) copy-start(s32[4,8]{1,0:T(4,128)} %param.34) | copy-start | bytes 388
  34.5 15.7 %copy-start.8 = (s32[8,2]{0,1:T(2,128)S(1)}, s32[8,2]{0,1:T(2,128)}, u32[]{:S(2)}) copy-start(s32[8,2]{0,1:T(2,128)} %constant.116.clone) | copy-start | bytes 196
  34.6 16.3 %copy-start.7 = (s32[8,4]{0,1:T(4,128)S(1)}, s32[8,4]{0,1:T(4,128)}, u32[]{:S(2)}) copy-start(s32[8,4]{0,1:T(4,128)} %constant.78.clone) | copy-start | bytes 388
  36.3 23.9 %collective-permute-start = (f32[8,4,432]{2,1,0:T(4,128)S(1)}, f32[8,4,432]{2,1,0:T(4,128)S(1)}, u32[]{:S(2)}, u32[]{:S(2)}) collective-permute-start(f32[8,4,432]{2,1,0:T(4,128)S(1)} %bitcast.53), channel_id=1, source_target_pairs={{0,1},{1,2},{2,3},{3,4},{4,5},{5,6},{6,7},{7,8},{8,9},{9,10},{10,1... | collective-permute-start | bytes 165896 | tf_op jit(solution)/shard_map/ppermute | solution.py:22
  39.3 20.9 %collective-permute-start.1 = (f32[8,4,432]{2,1,0:T(4,128)S(1)}, f32[8,4,432]{2,1,0:T(4,128)S(1)}, u32[]{:S(2)}, u32[]{:S(2)}) collective-permute-start(f32[8,4,432]{2,1,0:T(4,128)S(1)} %bitcast.54), channel_id=1, source_target_pairs={{0,15},{1,0},{2,1},{3,2},{4,3},{5,4},{6,5},{7,6},{8,7},{9,8},{10,9... | collective-permute-start | bytes 165896 | tf_op jit(solution)/shard_map/ppermute | solution.py:22
  43.4 16.9 %collective-permute-start.2 = (f32[8,4,432]{2,1,0:T(4,128)S(1)}, f32[8,4,432]{2,1,0:T(4,128)S(1)}, u32[]{:S(2)}, u32[]{:S(2)}) collective-permute-start(f32[8,4,432]{2,1,0:T(4,128)S(1)} %bitcast.55), channel_id=1, source_target_pairs={{0,16},{16,0},{1,17},{17,1},{2,18},{18,2},{3,19},{19,3},{4,20},{20... | collective-permute-start | bytes 165896 | tf_op jit(solution)/shard_map/ppermute | solution.py:22
  43.5 12.7 %collective-permute-start.6 = (f32[8,16]{1,0:T(8,128)S(1)}, f32[8,16]{1,0:T(8,128)S(1)}, u32[]{:S(2)}, u32[]{:S(2)}) collective-permute-start(f32[8,16]{1,0:T(8,128)S(1)} %mul.289), channel_id=1, source_target_pairs={{0,1},{1,2},{2,3},{3,4},{4,5},{5,6},{6,7},{7,8},{8,9},{9,10},{10,1... | collective-permute-start | bytes 1544 | tf_op jit(solution)/shard_map/ppermute | solution.py:22
  43.5 12.8 %collective-permute-start.7 = (f32[8,16]{1,0:T(8,128)S(1)}, f32[8,16]{1,0:T(8,128)S(1)}, u32[]{:S(2)}, u32[]{:S(2)}) collective-permute-start(f32[8,16]{1,0:T(8,128)S(1)} %mul.289), channel_id=1, source_target_pairs={{0,15},{1,0},{2,1},{3,2},{4,3},{5,4},{6,5},{7,6},{8,7},{9,8},{10,9... | collective-permute-start | bytes 1544 | tf_op jit(solution)/shard_map/ppermute | solution.py:22
  54.7 6.4 %copy-start.2 = (f32[16,12,1]{1,0,2:T(8,128)S(1)}, f32[16,12,1]{1,0,2:T(8,128)}, u32[]{:S(2)}) copy-start(f32[16,12,1]{1,0,2:T(8,128)} %constant.139) | copy-start | bytes 2308
  56.2 12.4 %copy-start.5 = (s32[4]{0:T(128)S(1)}, s32[4]{0:T(128)}, u32[]{:S(2)}) copy-start(s32[4]{0:T(128)} %constant.135) | copy-start | bytes 52
  56.2 13.1 %copy-start.4 = (s32[4]{0:T(128)S(1)}, s32[4]{0:T(128)}, u32[]{:S(2)}) copy-start(s32[4]{0:T(128)} %constant.136) | copy-start | bytes 52
  56.2 1.2 %collective-permute-start.8 = (f32[8,16]{1,0:T(8,128)S(1)}, f32[8,16]{1,0:T(8,128)S(1)}, u32[]{:S(2)}, u32[]{:S(2)}) collective-permute-start(f32[8,16]{1,0:T(8,128)S(1)} %mul.289), channel_id=1, source_target_pairs={{0,16},{16,0},{1,17},{17,1},{2,18},{18,2},{3,19},{19,3},{4,20},{20... | collective-permute-start | bytes 1544 | tf_op jit(solution)/shard_map/ppermute | solution.py:22
  61.6 12.1 %collective-permute-start.3 = (f32[8,16,432]{2,1,0:T(8,128)S(1)}, f32[8,16,432]{2,1,0:T(8,128)S(1)}, u32[]{:S(2)}, u32[]{:S(2)}) collective-permute-start(f32[8,16,432]{2,1,0:T(8,128)S(1)} %get-tuple-element.53), channel_id=1, source_target_pairs={{0,1},{1,2},{2,3},{3,4},{4,5},{5,6},{6,7},{7,8},{8,9},{9,10},{10,1... | collective-permute-start | bytes 663560 | tf_op jit(solution)/shard_map/ppermute | solution.py:22
  61.7 12.1 %collective-permute-start.4 = (f32[8,16,432]{2,1,0:T(8,128)S(1)}, f32[8,16,432]{2,1,0:T(8,128)S(1)}, u32[]{:S(2)}, u32[]{:S(2)}) collective-permute-start(f32[8,16,432]{2,1,0:T(8,128)S(1)} %get-tuple-element.53), channel_id=1, source_target_pairs={{0,15},{1,0},{2,1},{3,2},{4,3},{5,4},{6,5},{7,6},{8,7},{9,8},{10,9... | collective-permute-start | bytes 663560 | tf_op jit(solution)/shard_map/ppermute | solution.py:22
  70.5 3.4 %collective-permute-start.5 = (f32[8,16,432]{2,1,0:T(8,128)S(1)}, f32[8,16,432]{2,1,0:T(8,128)S(1)}, u32[]{:S(2)}, u32[]{:S(2)}) collective-permute-start(f32[8,16,432]{2,1,0:T(8,128)S(1)} %get-tuple-element.53), channel_id=1, source_target_pairs={{0,16},{16,0},{1,17},{17,1},{2,18},{18,2},{3,19},{19,3},{4,20},{20... | collective-permute-start | bytes 663560 | tf_op jit(solution)/shard_map/ppermute | solution.py:22
where the time goes:
time: 81.2 us; the launch traced here: 81 us
  other arithmetic  29.8 us (37%)
  local copies, waits for them, and re-layouts  26.6 us (33%)
  starting transfers between devices  18.5 us (23%)
  waiting for transfers between devices  4.19 us (5%)
  between operations  1.41 us (2%)
    ppermute x9, starting transfers between devices, passed_along(): return lax.ppermute(value, axis, pairs)  18.5 us
    add x2, other arithmetic, local(): current + mix_horiz * (east_side - 2.0 * current + west_side)  12.2 us
    unnamed x44, local copies, waits for them, and re-layouts  5.32 us
    ppermute x9, waiting for transfers between devices, passed_along(): return lax.ppermute(value, axis, pairs)  4.19 us
    slice x4, local copies, waits for them, and re-layouts, local(): level_above = jnp.concatenate([current[:, 1:], current[:, -1:]], axis=1)  3.5 us
    slice x4, local copies, waits for them, and re-layouts, local(): jnp.roll(current, -1, axis=2)  3.49 us
    sub x2, other arithmetic, local(): current = current + flux_up - flux_below  3.45 us
    slice x4, local copies, waits for them, and re-layouts, local(): jnp.roll(current, width - 1, axis=2)  3.44 us
  transfers between devices with their start and end apart: 9, of which 2 were waited for; matrix products, arithmetic and copies ran while one was open for 16% of the time, Pallas kernels for 0%

commit v1 on v0

v1 whole, which is shorter than its diff:
```python
import functools
import math

import jax
import jax.numpy as jnp
import numpy as np
from jax import lax
from jax.experimental import pallas as pl
from jax.experimental.pallas import tpu as pltpu
from jax.sharding import PartitionSpec as P

NSUB = 2
BLK_R = 4
BLK_C = 2
PER_TIME = 10.0
LANES = 128
HI = lax.Precision.HIGHEST
F32 = jnp.float32
BF16 = jnp.bfloat16
I32 = jnp.int32

CELL_EDGE = [[0, 1], [1, 3], [2, 3], [0, 2]]
GLL_EDGE = [[0, 1, 2, 3], [3, 7, 11, 15], [12, 13, 14, 15], [0, 4, 8, 12]]


def lagrange(q, z):
    centres = [-1.5, -0.5, 0.5, 1.5]
    product = 1.0
    for r in range(4):
        if r != q:
            product = product * (z - centres[r]) / (centres[q] - centres[r])
    return product


def linear_weight(j, z):
    return 0.5 - z if j == 0 else 0.5 + z


GLL_NODES = [-1.0, -1.0 / math.sqrt(5.0), 1.0 / math.sqrt(5.0), 1.0]


def remap_matrix():
    matrix = [[0.0 for column in range(12)] for row in range(16)]
    for b in range(4):
        for a in range(4):
            p = 4 * b + a
            x = GLL_NODES[a]
            y = GLL_NODES[b]
            for j in range(2):
                for i in range(2):
                    matrix[p][2 * j + i] += 0.5 * linear_weight(j, y) * lagrange(
                        1 + i, x
                    ) + 0.5 * linear_weight(i, x) * lagrange(1 + j, y)
            for m in range(2):
                matrix[p][4 + 6 + m] += 0.5 * linear_weight(m, y) * lagrange(0, x)
                matrix[p][4 + 2 + m] += 0.5 * linear_weight(m, y) * lagrange(3, x)
                matrix[p][4 + 0 + m] += 0.5 * linear_weight(m, x) * lagrange(0, y)
                matrix[p][4 + 4 + m] += 0.5 * linear_weight(m, x) * lagrange(3, y)
    return np.array(matrix, np.float32)


class Sizes:
    def __init__(self, elements, flat_len):
        self.elements = elements
        self.edges = 4 * elements
        self.cells = 4 * elements
        self.points = 16 * elements
        self.raw = 2 * BLK_R
        self.part = 4 * BLK_R
        self.flat = flat_len
        self.wide = -(-(flat_len + 2) // LANES) * LANES
        self.columns = 2 * self.cells + 4 * self.raw
        self.ops = self.columns + 8
        self.face_rows = self.cells + 2 * self.raw + 8
        self.tile_rows = 2 * self.raw + self.part


def constant_tables(size):
    matrix = remap_matrix()
    across_t = np.zeros((2 * size.edges, size.points), np.float32)
    own_t = np.zeros((size.cells, size.points), np.float32)
    spread_t = np.zeros((4 * size.edges, size.points), np.float32)
    for e in range(size.elements):
        for p in range(16):
            for c in range(4):
                own_t[4 * e + c, 16 * e + p] = matrix[p][c]
            for k in range(4):
                for m in range(2):
                    row = m * size.edges + k * size.elements + e
                    across_t[row, 16 * e + p] = matrix[p][4 + 2 * k + m]
        for k in range(4):
            for t in range(4):
                row = t * size.edges + k * size.elements + e
                spread_t[row, 16 * e + GLL_EDGE[k][t]] = 1.0
    return np.concatenate([across_t, own_t, spread_t], axis=0)


def edge_weight(t, m):
    return 0.5 * linear_weight(m, GLL_NODES[t]) * lagrange(0, -1.0)


def iota(shape, dim):
    return lax.broadcasted_iota(I32, shape, dim)


def dot_nn(a, b, precision=HI):
    return lax.dot_general(
        a, b, (((1,), (0,)), ((), ())), precision=precision, preferred_element_type=F32
    )


def dot_nt(a, b, precision=HI):
    return lax.dot_general(
        a, b, (((1,), (1,)), ((), ())), precision=precision, preferred_element_type=F32
    )


def dot_tn(a, b, precision=HI):
    return lax.dot_general(
        a, b, (((0,), (0,)), ((), ())), precision=precision, preferred_element_type=F32
    )


def flat_row(table):
    return jnp.concatenate([table[k : k + 1, :] for k in range(4)], axis=1)


def twice(row):
    return jnp.concatenate([row, row], axis=1)


def side_slots(size, side, order):
    n = size.edges
    key = jnp.where(side >= 0, side * 2 * n + order, 8 * n)
    eye = iota((n, n), 0) == iota((n, n), 1)
    wide = jnp.broadcast_to(key.astype(F32), (n, n))
    column = jnp.sum(jnp.where(eye, wide, 0.0), axis=1, keepdims=True)
    floor = jnp.broadcast_to((side * 2 * n).astype(F32), (n, n))
    lower = jnp.logical_and(column < wide, column >= floor)
    count = jnp.sum(jnp.where(lower, 1.0, 0.0), axis=0, keepdims=True).astype(I32)
    return jnp.where(side >= 0, count, 0)


def edge_cell(k, m):
    odd = k & 1
    base = jnp.where(k == 2, 2, odd * jnp.where(k == 1, 1, 0))
    return base + m * (1 + odd)


def edge_point(k, t):
    odd = k & 1
    base = jnp.where(k == 2, 12, jnp.where(k == 1, 3, 0))
    return base + t * (1 + 3 * odd)


class Edges:
    def __init__(self, size, slots_row, codes_row, parity):
        n = size.edges
        flat = iota((1, n), 1)
        self.k = flat // size.elements
        self.e = flat % size.elements
        self.source = slots_row // size.elements
        self.place = slots_row % size.elements
        self.other_k = codes_row // 2
        self.turned = codes_row % 2
        self.side = jnp.where(
            self.source == 2 - parity, 0, jnp.where(self.source == 1 + parity, 1, -1)
        )
        self.flat = flat
        self.other_flat = self.other_k * size.elements + self.place


def gather_matrix_t(size, edges, slot, twin):
    cells, raw = size.cells, size.raw
    rows = []
    for m in range(2):
        mm = jnp.where(edges.turned == 1, 1 - m, m)
        cell = 4 * edges.place + edge_cell(edges.other_k, mm)
        local = jnp.where(edges.source == 0, cells * twin, cells * (1 - twin)) + cell
        far = 2 * cells + 2 * raw * edges.side + raw * twin + 2 * slot + mm
        rows.append(jnp.where(edges.side >= 0, far, local))
    target = jnp.concatenate(rows, axis=1)
    return jnp.where(iota((size.columns, 2 * size.edges), 0) == target, 1.0, 0.0)


def operator_t(size, tables, gather_t, mass_row, twin):
    across_t = tables[0 : 2 * size.edges, :]
    own_t = tables[2 * size.edges : 2 * size.edges + size.cells, :]
    from_across = dot_nn(gather_t, across_t)
    zero = jnp.zeros((size.cells, size.points), F32)
    placed = [zero, own_t] if twin else [own_t, zero]
    rest = jnp.zeros((size.columns - 2 * size.cells, size.points), F32)
    full = from_across + jnp.concatenate(placed + [rest], axis=0)
    tail = jnp.where(iota((8, size.points), 0) == 0, 1.0, 0.0)
    return jnp.concatenate([full, tail], axis=0) * mass_row


def spread_of(size, tables):
    start = 2 * size.edges + size.cells
    return tables[start : start + 4 * size.edges, :]


def crm_kernel(
    size,
    levels,
    width,
    state_ref,
    active_ref,
    mix_ref,
    drift_ref,
    cond_ref,
    mixz_ref,
    slots_ref,
    codes_ref,
    mass_ref,
    new_ref,
    face_ref,
    in_buf,
    out_buf,
    in_sem,
    out_sem,
):
    fields = in_buf.shape[1]
    per_lane = LANES // width

    def load(e):
        return pltpu.make_async_copy(
            state_ref.at[:, :, pl.ds(e * LANES, LANES)], in_buf.at[e], in_sem.at[e]
        )

    def save(e):
        return pltpu.make_async_copy(
            out_buf.at[e], new_ref.at[:, :, pl.ds(e * LANES, LANES)], out_sem.at[e]
        )

    for e in range(size.elements):
        load(e).start()

    eye = iota((levels, levels), 0) == iota((levels, levels), 1)
    mixz = jnp.broadcast_to(mixz_ref[...], (levels, levels))
    couple = jnp.sum(jnp.where(eye, mixz, 0.0), axis=1, keepdims=True)
    couple = jnp.where(iota((levels, 1), 0) < levels - 1, couple, 0.0)
    couple = jnp.broadcast_to(couple, (levels, LANES))
    level = iota((levels, LANES), 0)
    lane = iota((1, LANES), 1)
    group = lane // width
    at_last = jnp.broadcast_to(lane % width == width - 1, (levels, LANES))
    at_first = jnp.broadcast_to(lane % width == 0, (levels, LANES))

    def lanes_of(ref, e):
        row = jnp.full((1, LANES), ref[e * per_lane], ref.dtype)
        for c in range(1, per_lane):
            row = jnp.where(group == c, ref[e * per_lane + c], row)
        return row

    def element(e):
        load(e).wait()
        mix = lanes_of(mix_ref, e)
        half = 0.5 * lanes_of(drift_ref, e)
        rate = jnp.broadcast_to(lanes_of(cond_ref, e), (levels, LANES))
        alive = level < lanes_of(active_ref, e)
        centre = jnp.broadcast_to(1.0 - 2.0 * mix, (levels, LANES))
        east_c = jnp.broadcast_to(mix - half, (levels, LANES))
        west_c = jnp.broadcast_to(mix + half, (levels, LANES))

        def transport(a):
            east = jnp.where(
                at_last, pltpu.roll(a, width - 1, 1), pltpu.roll(a, LANES - 1, 1)
            )
            west = jnp.where(
                at_first, pltpu.roll(a, LANES - width + 1, 1), pltpu.roll(a, 1, 1)
            )
            a = centre * a + east_c * east + west_c * west
            flux = couple * (pltpu.roll(a, levels - 1, 0) - a)
            return a + flux - pltpu.roll(flux, 1, 0)

        start = [in_buf[e, f].astype(F32) for f in range(fields)]
        cur = list(start)
        for substep in range(NSUB):
            cur = [transport(a) for a in cur]
            t, qv, ql, qi = cur[:4]
            sat = 0.5 * jnp.exp(0.3 * t)
            cond = jnp.where(alive, jnp.maximum(rate * (qv - sat), -ql), 0.0)
            qv = qv - cond
            ql = ql + cond
            t = t + 0.5 * cond
            freeze = jnp.where(alive, 0.15 * ql * (1.0 - jnp.tanh(t)), 0.0)
            ql = ql - freeze
            qi = qi + freeze
            t = t + 0.1 * freeze
            cur[:4] = [t, qv, ql, qi]
        for f in range(fields):
            out_buf[e, f] = cur[f].astype(BF16)
        save(e).start()
        return jnp.concatenate([cur[f] - start[f] for f in range(fields)], axis=0)

    pair_lanes = 2 * LANES
    cell_of = iota((2 * per_lane, pair_lanes), 1) // width
    mean = jnp.where(iota((2 * per_lane, pair_lanes), 0) == cell_of, PER_TIME / width, 0.0)
    mean = mean.astype(BF16)
    face_ref[...] = jnp.zeros(face_ref.shape, F32)

    def pair(i, carry):
        diff = jnp.concatenate([element(2 * i), element(2 * i + 1)], axis=1)
        high = diff.astype(BF16)
        low = (diff - high.astype(F32)).astype(BF16)
        rows = dot_nt(mean, high, None) + dot_nt(mean, low, None)
        face_ref[pl.ds(pl.multiple_of(i * 2 * per_lane, 8), 2 * per_lane), 0 : size.flat] = rows
        return carry

    lax.fori_loop(0, size.elements // 2, pair, 0)

    parity = lax.axis_index("tile") % 2
    slots_row = flat_row(slots_ref[...])
    codes_row = flat_row(codes_ref[...])
    edges = Edges(size, slots_row, codes_row, parity)
    slot = side_slots(size, edges.side, edges.flat)
    rows = 2 * size.raw
    place = jnp.where(edges.side >= 0, edges.side * size.raw + 2 * slot, -8)
    put = jnp.concatenate([place, place + 1], axis=1)
    select = jnp.where(iota((rows, 2 * size.edges), 0) == put, 1.0, 0.0)
    cell = jnp.concatenate(
        [4 * edges.e + edge_cell(edges.k, m) for m in range(2)], axis=1
    )
    cell_t = jnp.where(iota((size.cells, 2 * size.edges), 0) == cell, 1.0, 0.0)
    pick = dot_nt(select, cell_t, None)
    face_ref[size.cells : size.cells + rows, :] = dot_nn(pick, face_ref[0 : size.cells, :])
    base = size.cells + rows
    face_ref[base : base + 1, 0 : size.edges] = slots_row.astype(F32)
    face_ref[base + 1 : base + 2, 0 : size.edges] = codes_row.astype(F32)
    face_ref[base + 2 : base + 3, 0 : size.points] = mass_ref[...]

    for e in range(size.elements):
        save(e).wait()


def weights_kernel(size, slots_ref, codes_ref, mass_ref, table_ref, part_ref):
    parity = lax.axis_index("tile") % 2
    edges = Edges(size, flat_row(slots_ref[...]), flat_row(codes_ref[...]), parity)
    tables = table_ref[...]
    slot_far = side_slots(size, edges.side, edges.other_flat)
    oper_t = operator_t(
        size, tables, gather_matrix_t(size, edges, slot_far, 0), mass_ref[...], False
    )
    slot = side_slots(size, edges.side, edges.flat)
    rows = 2 * size.part
    first = jnp.where(edges.side >= 0, edges.side * size.part + 4 * slot, -8)
    put = jnp.concatenate([first + t for t in range(4)], axis=1)
    select = jnp.where(iota((rows, 4 * size.edges), 0) == put, 1.0, 0.0)
    points = dot_nn(select, spread_of(size, tables), None)
    part = dot_nt(points, oper_t)
    n = size.elements
    both = jnp.zeros((1, n), I32)
    hits = []
    for s in range(2):
        hit = jnp.where(edges.side == s, 1, 0)
        total = hit[:, 0:n]
        for k in range(1, 4):
            total = total + hit[:, k * n : (k + 1) * n]
        hits.append(total)
    both = jnp.where(jnp.logical_and(hits[0] > 0, hits[1] > 0), 1.0, 0.0)
    flag = jnp.max(both)
    part_ref[:, 0 : size.ops] = part
    part_ref[:, size.ops :] = jnp.full((rows, LANES - size.ops), flag, F32)


def message_kernel(size, own_ref, twin_ref, part_ref, even_ref, odd_ref):
    cells = jnp.concatenate([own_ref[0 : size.cells, :], twin_ref[0 : size.cells, :]], axis=0)
    part = dot_nn(part_ref[:, 0 : 2 * size.cells], cells)
    lane = iota((2 * size.part, size.wide), 1)
    part = jnp.where(lane == size.flat, part_ref[:, size.columns : size.columns + 1], part)
    part = jnp.where(lane == size.flat + 1, part_ref[:, size.ops : size.ops + 1], part)
    for s, ref in enumerate((even_ref, odd_ref)):
        first = size.cells + s * size.raw
        ref[0 : size.raw, :] = own_ref[first : first + size.raw, :]
        ref[size.raw : 2 * size.raw, :] = twin_ref[first : first + size.raw, :]
        ref[2 * size.raw :, :] = part[s * size.part : (s + 1) * size.part, :]


def inner_kernel(
    size,
    slots_ref,
    codes_ref,
    mass_ref,
    table_ref,
    own_ref,
    twin_ref,
    sum_ref,
    near_ref,
    matrix_ref,
):
    parity = lax.axis_index("tile") % 2
    tables = table_ref[...]
    base = size.cells + 2 * size.raw
    own = Edges(size, flat_row(slots_ref[...]), flat_row(codes_ref[...]), parity)
    twin = Edges(
        size,
        twin_ref[base : base + 1, 0 : size.edges].astype(I32),
        twin_ref[base + 1 : base + 2, 0 : size.edges].astype(I32),
        parity,
    )
    twin_mass = twin_ref[base + 2 : base + 3, 0 : size.points]
    own_slot = side_slots(size, own.side, own.other_flat)
    twin_slot = side_slots(size, twin.side, twin.other_flat)
    oper = jnp.concatenate(
        [
            operator_t(size, tables, gather_matrix_t(size, own, own_slot, 0), mass_ref[...], False),
            operator_t(size, tables, gather_matrix_t(size, twin, twin_slot, 1), twin_mass, True),
        ],
        axis=1,
    )
    far = 2 * size.points
    targets = []
    for t in range(4):
        tt = jnp.where(own.turned == 1, 3 - t, t)
        point = 16 * own.place + edge_point(own.other_k, tt)
        local = jnp.where(own.source == 0, 0, size.points) + point
        targets.append(
            jnp.where(own.side >= 0, far + own.side * size.part + 4 * own_slot + tt, local)
        )
    target = jnp.concatenate(targets, axis=1)
    rows = far + 2 * size.part
    partner_t = jnp.where(iota((rows, 4 * size.edges), 0) == target, 1.0, 0.0)
    assemble_t = dot_nn(partner_t, spread_of(size, tables), None)
    eye = jnp.where(iota((far, size.points), 0) == iota((far, size.points), 1), 1.0, 0.0)
    total_t = dot_nn(oper, assemble_t[0:far, :] + eye)
    cells = 2 * size.cells
    matrix_ref[0 : 4 * size.raw, :] = total_t[cells : size.columns, :]
    matrix_ref[4 * size.raw : 4 * size.raw + 2 * size.part, :] = assemble_t[far:, :]
    matrix_ref[4 * size.raw + 2 * size.part :, :] = total_t[size.columns :, :]
    chip = jnp.concatenate([own_ref[0 : size.cells, :], twin_ref[0 : size.cells, :]], axis=0)
    sum_ref[...] = dot_tn(chip[:, 0 : size.flat], total_t[0:cells, :])
    side_slot = jnp.where(own.side >= 0, own.side * BLK_R + own_slot, -1)
    match = jnp.broadcast_to(twice(side_slot), (2 * size.part, 2 * size.edges)) == (
        iota((2 * size.part, 2 * size.edges), 0) // 4
    )
    t_of = iota((2 * size.part, 2 * size.edges), 0) % 4
    m_of = iota((2 * size.part, 2 * size.edges), 1) // size.edges
    weight = jnp.zeros(match.shape, F32)
    for t in range(4):
        for m in range(2):
            here = jnp.logical_and(t_of == t, m_of == m)
            weight = jnp.where(here, edge_weight(t, m), weight)
    weight = jnp.where(match, weight, 0.0)
    cell = jnp.concatenate(
        [
            4 * own.e + edge_cell(own.k, jnp.where(own.turned == 1, 1 - m, m))
            for m in range(2)
        ],
        axis=1,
    )
    cell_t = jnp.where(iota((size.cells, 2 * size.edges), 0) == cell, 1.0, 0.0)
    near_ref[...] = dot_nn(dot_nt(weight, cell_t), own_ref[0 : size.cells, :])


def final_kernel(size, even_ref, odd_ref, sum_ref, near_ref, matrix_ref, out_ref, keep_ref):
    raw = 2 * size.raw
    mass = jnp.concatenate(
        [ref[raw:, size.flat : size.flat + 1] for ref in (even_ref, odd_ref)], axis=0
    )
    part = jnp.concatenate([even_ref[raw:, :], odd_ref[raw:, :]], axis=0)
    part = part + mass * near_ref[...]
    rows = jnp.concatenate([even_ref[0:raw, :], odd_ref[0:raw, :], part], axis=0)
    n = 2 * raw + 2 * size.part
    side = matrix_ref[2 * raw : n, :]
    total = sum_ref[...] + dot_tn(rows[:, 0 : size.flat], matrix_ref[0:n, :])
    mass_sum = matrix_ref[n : n + 1, :] + jnp.sum(side * mass, axis=0, keepdims=True)
    out_ref[...] = total / mass_sum
    keep_ref[0:1, :] = mass_sum
    row = jnp.concatenate(
        [ref[raw : raw + 1, size.flat + 1 : size.flat + 2] for ref in (even_ref, odd_ref)], axis=0
    )
    keep_ref[1:3, :] = jnp.broadcast_to(row, (2, size.points))
    keep_ref[3:, :] = jnp.zeros((5, size.points), F32)


VMEM = pl.BlockSpec(memory_space=pltpu.VMEM)
SMEM = pl.BlockSpec(memory_space=pltpu.SMEM)
ANY = pl.BlockSpec(memory_space=pl.ANY)


def call(body, name, outs, ins, in_specs=None, out_specs=None, scratch=(), limit=8):
    return pl.pallas_call(
        body,
        out_shape=outs,
        in_specs=in_specs or [VMEM] * len(ins),
        out_specs=out_specs or [VMEM] * len(outs),
        scratch_shapes=scratch,
        compiler_params=pltpu.CompilerParams(vmem_limit_bytes=limit * 1024 * 1024),
        name=name,
    )(*ins)


def shape_of(*dims):
    return jax.ShapeDtypeStruct(dims, F32)


def advance(size, crm_state, column_args, mix_z, slots, codes, mass_row):
    fields, levels, lanes = crm_state.shape
    width = lanes // column_args[0].shape[0]
    buffers = (size.elements, fields, levels, LANES)
    return call(
        functools.partial(crm_kernel, size, levels, width),
        "advance",
        [jax.ShapeDtypeStruct(crm_state.shape, BF16), shape_of(size.face_rows, size.wide)],
        [crm_state, *column_args, mix_z.reshape(1, levels), slots, codes, mass_row],
        in_specs=[ANY] + [SMEM] * 4 + [VMEM] * 4,
        out_specs=[ANY, VMEM],
        scratch=[
            pltpu.VMEM(buffers, BF16),
            pltpu.VMEM(buffers, BF16),
            pltpu.SemaphoreType.DMA((size.elements,)),
            pltpu.SemaphoreType.DMA((size.elements,)),
        ],
        limit=16,
    )


def swap_pairs(odd):
    tiles = lax.axis_size("tile")
    pairs = []
    for t in range(tiles):
        up = (t % 2 == 0) != odd
        pairs.append((t, (t + 1 if up else t - 1) % tiles))
    return pairs


def swap(value, odd):
    return lax.ppermute(value, "tile", swap_pairs(odd))


def shift(value, axis, steps):
    count = lax.axis_size(axis)
    return lax.ppermute(value, axis, [(s, (s + steps) % count) for s in range(count)])


def assemble_pair(size, face, slots, codes, mass_row):
    tables = jnp.asarray(constant_tables(size))
    twin = shift(face, "face", 1)
    (part,) = call(
        functools.partial(weights_kernel, size),
        "weights",
        [shape_of(2 * size.part, LANES)],
        [slots, codes, mass_row, tables],
    )
    message = shape_of(size.tile_rows, size.wide)
    even, odd = call(
        functools.partial(message_kernel, size), "message", [message] * 2, [face, twin, part]
    )
    odd_in = swap(odd, True)
    even_in = swap(even, False)
    extra = 4 * size.raw + 2 * size.part
    inner, near, matrix = call(
        functools.partial(inner_kernel, size),
        "inner",
        [
            shape_of(size.flat, size.points),
            shape_of(2 * size.part, size.wide),
            shape_of(extra + 8, size.points),
        ],
        [slots, codes, mass_row, tables, face, twin],
    )
    out, keep = call(
        functools.partial(final_kernel, size),
        "final",
        [shape_of(size.flat, size.points), shape_of(8, size.points)],
        [even_in, odd_in, inner, near, matrix],
    )
    return out, part, keep, matrix, even_in, odd_in


def second_exchange(size, out, part, keep, matrix, even_in, odd_in):
    raw = 2 * size.raw
    mine = part[0, size.ops] > 0.0
    inputs = (even_in, odd_in)
    for s in range(2):
        source = inputs[1 - s]
        first = 2 * size.cells + raw * (1 - s)
        weights = part[s * size.part : (s + 1) * size.part, first : first + raw]
        side = matrix[2 * raw + s * size.part : 2 * raw + (s + 1) * size.part, :]
        wanted = jnp.logical_or(mine, keep[1 + s, 0] > 0.0)

        def add(value, s=s, source=source, weights=weights, side=side):
            sent = jnp.dot(weights, source[0:raw, 0 : size.flat], precision=HI)
            got = swap(sent, s == 1)
            return value + jnp.dot(got.T, side, precision=HI) / keep[0:1, :]

        out = lax.cond(wanted, add, lambda value: value, out)
    return out


def local(
    crm_state,
    active_levels,
    mix_x,
    drift_speed,
    cond_rate,
    mix_z,
    point_mass,
    neighbor_slots,
    edge_codes,
):
    fields, levels, _ = crm_state.shape
    size = Sizes(neighbor_slots.shape[1], fields * levels)
    mass_row = point_mass.reshape(1, size.points)
    new_state, face = advance(
        size,
        crm_state,
        (active_levels, mix_x, drift_speed, cond_rate),
        mix_z,
        neighbor_slots,
        edge_codes,
        mass_row,
    )
    results = assemble_pair(size, face, neighbor_slots, edge_codes, mass_row)
    out = second_exchange(size, *results)
    return (new_state, out.reshape(fields, levels, size.points))


def solution(mesh):
    in_specs = (
        P(None, None, ("face", "tile")),
        P(("face", "tile")),
        P(("face", "tile")),
        P(("face", "tile")),
        P(("face", "tile")),
        P(),
        P(("face", "tile")),
        P(None, ("face", "tile")),
        P(None, ("face", "tile")),
    )
    out_specs = (P(None, None, ("face", "tile")), P(None, None, ("face", "tile")))
    return jax.shard_map(local, mesh=mesh, in_specs=in_specs, out_specs=out_specs, check_vma=False)
```

time: 81.2 us -> 27.4 us (0.34)
  other arithmetic: 29.8 us -> 0 us
  local copies, waits for them, and re-layouts: 26.6 us -> 6.28 us
  starting transfers between devices: 18.5 us -> 7.99 us
  Pallas kernels: 0 us -> 9.01 us
  waiting for transfers between devices: 4.19 us -> 1.24 us
  between operations: 1.41 us -> 2.67 us
    add x6 -> x0, other arithmetic: 12.2 us -> none  [the longest x2 12.2 us: local(): current + mix_horiz * (east_side - 2.0 * current + west_side)]
    ppermute x9 -> x3, starting transfers between devices: 18.5 us -> 7.99 us  [the longest x2 7.43 us: swap(): return lax.ppermute(value, 'tile', swap_pairs(odd))]
    slice x17 -> x2, local copies, waits for them, and re-layouts: 10.8 us -> 1.11 us  [the longest x1 0.58 us: second_exchange(): mine = part[0, size.ops] > 0.0]
    pallas_call x0 -> x5, Pallas kernels: none -> 9.01 us  [call(): pl.pallas_call(body, out_shape=outs, in_specs=in_specs or [VMEM] * len(in...]
    gather x11 -> x0, local copies, waits for them, and re-layouts: 6.55 us -> none  [the longest x4 2.7 us: local(): jnp.take(flat_mass, point_index).reshape(element_count, 4)]
    scatter-add x8 -> x0, other arithmetic: 5.1 us -> none  [the longest x4 2.65 us: local(): numerator.at[:, GLL_EDGE[k]]]
    sub x2 -> x0, other arithmetic: 3.45 us -> none  [local(): current = current + flux_up - flux_below]
    ppermute x9 -> x3, waiting for transfers between devices: 4.19 us -> 1.24 us  [the longest x2 0.87 us: swap(): return lax.ppermute(value, 'tile', swap_pairs(odd))]
  transfers between devices with their start and end apart: 9 -> 3, of which waited for: 2 -> 2; matrix products, arithmetic and copies ran while one was open for 16% -> 2% of each run, Pallas kernels for 0% -> 7%
where the time goes in v1:
time: 27.4 us; the launch traced here: 27.2 us
  Pallas kernels  9.01 us (33%)
  starting transfers between devices  7.99 us (29%)
  local copies, waits for them, and re-layouts  6.28 us (23%)
  between operations  2.67 us (10%)
  waiting for transfers between devices  1.24 us (5%)
    pallas_call x5, Pallas kernels, call(): pl.pallas_call(body, out_shape=outs, in_specs=in_specs or [VMEM] * len(in...  9.01 us
    ppermute x2, starting transfers between devices, swap(): return lax.ppermute(value, 'tile', swap_pairs(odd))  7.43 us
    unnamed x22, local copies, waits for them, and re-layouts  5.17 us
    ppermute x2, waiting for transfers between devices, swap(): return lax.ppermute(value, 'tile', swap_pairs(odd))  0.87 us
    slice x1, local copies, waits for them, and re-layouts, second_exchange(): mine = part[0, size.ops] > 0.0  0.58 us
    ppermute x1, starting transfers between devices, shift(): lax.ppermute(value, axis, [(s, (s + steps) % count) for s in range(count)])  0.56 us
  transfers between devices with their start and end apart: 3, of which 2 were waited for; matrix products, arithmetic and copies ran while one was open for 2% of the time, Pallas kernels for 7%

profile of v1, /device:TPU:0, one launch (start us, length us, event | category | flops | bytes accessed | tf_op | source)
XLA Modules:
  0.0 27.2 jit_solution(8105640782792584445)
XLA Ops:
  0.6 0.0 copy-start.2
  0.7 0.6 %copy-done.2 = s32[4,8]{1,0:T(4,128)S(1)} copy-done((s32[4,8]{1,0:T(4,128)S(1)}, s32[4,8]{1,0:T(4,128)}, u32[]{:S(2)}) %copy-start.2) | copy-done | bytes 152
  1.3 0.0 copy-done.6
  1.3 1.2 %copy-done = bf16[6,72,1024]{2,1,0:T(8,128)(2,1)S(1)} copy-done((bf16[6,72,1024]{2,1,0:T(8,128)(2,1)S(1)}, bf16[6,72,1024]{2,1,0:T(8,128)(2,1)}, u32[]{:S(2)}) %copy-start) | copy-done | bytes 884760
  2.5 0.7 %copy-done.3 = s32[4,8]{1,0:T(4,128)S(1)} copy-done((s32[4,8]{1,0:T(4,128)S(1)}, s32[4,8]{1,0:T(4,128)}, u32[]{:S(2)}) %copy-start.3) | copy-done | bytes 152
  3.2 0.7 %copy-done.7 = f32[32]{0:T(128)S(1)} copy-done((f32[32]{0:T(128)S(1)}, f32[32]{0:T(128)}, u32[]{:S(2)}) %copy-start.7) | copy-done | bytes 152
  3.8 0.7 %copy-done.8 = f32[32]{0:T(128)S(1)} copy-done((f32[32]{0:T(128)S(1)}, f32[32]{0:T(128)}, u32[]{:S(2)}) %copy-start.8) | copy-done | bytes 152
  4.5 0.7 %copy-done.9 = f32[72]{0:T(128)S(1)} copy-done((f32[72]{0:T(128)S(1)}, f32[72]{0:T(128)}, u32[]{:S(2)}) %copy-start.9) | copy-done | bytes 312
  5.2 6.6 %advance.1 = (bf16[6,72,1024]{2,1,0:T(8,128)(2,1)}, f32[56,512]{1,0:T(8,128)S(1)}) custom-call(bf16[6,72,1024]{2,1,0:T(8,128)(2,1)S(1)} %copy-done, s32[32]{0:T(128)S(1)} %copy-done.5, f32[32]{0:T(128)S(1)} %copy-done.6, f32[32]{0:T(128)S(1)} %copy-done.7, f32[32]{0:T(128)S(1)} %copy-done.8, f32[1,72]{1,0:T(1,128)S(1)} %bitcast.15, s32[4,8]{1,0:T(4,128)S(1)} %copy-done.2, ...), custom_call_target="tpu_custom_call" | custom-call | tf_op jit(solution)/shard_map/advance/pallas_call | solution.py:483
  11.7 0.6 %collective-permute-start.2 = (f32[56,512]{1,0:T(8,128)S(1)}, f32[56,512]{1,0:T(8,128)S(1)}, u32[]{:S(2)}, u32[]{:S(2)}) collective-permute-start(f32[56,512]{1,0:T(8,128)S(1)} %get-tuple-element.58.own_ref), channel_id=1, source_target_pairs={{0,16},{16,0},{1,17},{17,1},{2,18},{18,2},{3,19},{19,3},{4,20},{20... | collective-permute-start | bytes 344072 | tf_op jit(solution)/shard_map/ppermute | solution.py:534
  12.3 0.0 copy-done.1
  12.3 0.6 %weights.1.part_ref = f32[32,128]{1,0:T(8,128)S(1)} custom-call(s32[4,8]{1,0:T(4,128)S(1)} %copy-done.2, s32[4,8]{1,0:T(4,128)S(1)} %copy-done.3, f32[1,128]{1,0:T(1,128)S(1)} %bitcast.13, f32[224,128]{1,0:T(8,128)S(1)} %copy-done.1), custom_call_target="tpu_custom_call" | custom-call | tf_op jit(solution)/shard_map/weights/pallas_call | solution.py:483
  12.9 0.4 %collective-permute-done.2.twin_ref = f32[56,512]{1,0:T(8,128)S(1)} collective-permute-done((f32[56,512]{1,0:T(8,128)S(1)}, f32[56,512]{1,0:T(8,128)S(1)}, u32[]{:S(2)}, u32[]{:S(2)}) %collective-permute-start.2) | collective-permute-done | bytes 114720 | tf_op jit(solution)/shard_map/ppermute | solution.py:534
  13.2 0.2 message.1
  13.4 2.9 %collective-permute-start.3 = (f32[32,512]{1,0:T(8,128)S(1)}, f32[32,512]{1,0:T(8,128)S(1)}, u32[]{:S(2)}, u32[]{:S(2)}) collective-permute-start(f32[32,512]{1,0:T(8,128)S(1)} %get-tuple-element.59), channel_id=1, source_target_pairs={{0,1},{1,0},{2,3},{3,2},{4,5},{5,4},{6,7},{7,6},{8,9},{9,8},{10,11... | collective-permute-start | bytes 196616 | tf_op jit(solution)/shard_map/ppermute | solution.py:529
  16.3 4.5 %collective-permute-start.4 = (f32[32,512]{1,0:T(8,128)S(1)}, f32[32,512]{1,0:T(8,128)S(1)}, u32[]{:S(2)}, u32[]{:S(2)}) collective-permute-start(f32[32,512]{1,0:T(8,128)S(1)} %get-tuple-element.60), channel_id=1, source_target_pairs={{0,15},{1,2},{2,1},{3,4},{4,3},{5,6},{6,5},{7,8},{8,7},{9,10},{10,... | collective-permute-start | bytes 196616 | tf_op jit(solution)/shard_map/ppermute | solution.py:529
  20.9 0.6 %slice.42 = f32[1,1]{1,0:T(1,128)} slice(f32[32,128]{1,0:T(8,128)S(1)} %weights.1.part_ref), slice={[0:1], [104:105]} | slice | bytes 8 | tf_op jit(solution)/shard_map/slice | solution.py:574
  22.1 1.2 %inner.1 = (f32[432,128]{1,0:T(8,128)S(1)}, f32[32,512]{1,0:T(8,128)S(1)}, f32[72,128]{1,0:T(8,128)S(1)}) custom-call(s32[4,8]{1,0:T(4,128)S(1)} %copy-done.2, s32[4,8]{1,0:T(4,128)S(1)} %copy-done.3, f32[1,128]{1,0:T(1,128)S(1)} %bitcast.14, f32[224,128]{1,0:T(8,128)S(1)} %copy-done.1, f32[56,512]{1,0:T(8,128)S(1)} %get-tuple-element.58.own_ref, ...), custom_call_target="tpu_custom_call" | custom-call | tf_op jit(solution)/shard_map/inner/pallas_call | solution.py:483
  23.3 0.0 collective-permute-done.3.even_ref
  23.3 0.9 %collective-permute-done.4.odd_ref = f32[32,512]{1,0:T(8,128)S(1)} collective-permute-done((f32[32,512]{1,0:T(8,128)S(1)}, f32[32,512]{1,0:T(8,128)S(1)}, u32[]{:S(2)}, u32[]{:S(2)}) %collective-permute-start.4) | collective-permute-done | bytes 65568 | tf_op jit(solution)/shard_map/ppermute | solution.py:529
  24.2 0.4 %final.1 = (f32[432,128]{1,0:T(8,128)S(1)}, f32[8,128]{1,0:T(8,128)S(1)}) custom-call(f32[32,512]{1,0:T(8,128)S(1)} %collective-permute-done.3.even_ref, f32[32,512]{1,0:T(8,128)S(1)} %collective-permute-done.4.odd_ref, f32[432,128]{1,0:T(8,128)S(1)} %get-tuple-element.61.sum_ref, f32[32,512]{1,0:T(8,128)S(1)} %get-tuple-element.62.near_ref, ...), custom_call_target="tpu_custom_call" | custom-call | tf_op jit(solution)/shard_map/final/pallas_call | solution.py:483
  24.6 0.5 %fusion.10 = (f32[1,1]{1,0:T(1,128)}, f32[1,1]{1,0:T(1,128)}) fusion(f32[8,128]{1,0:T(8,128)S(1)} %get-tuple-element.76), kind=kLoop, calls=%fused_computation.14 | loop fusion | bytes 16 | tf_op jit(solution)/shard_map/slice | solution.py:581
  26.5 0.0 copy-start.10
  26.5 0.7 %copy-done.10 = f32[6,72,128]{2,1,0:T(8,128)} copy-done((f32[6,72,128]{2,1,0:T(8,128)}, f32[6,72,128]{2,1,0:T(8,128)S(1)}, u32[]{:S(2)}) %copy-start.10) | copy-done | bytes 221208
  (13 shorter events, 0.0 us)
Async XLA Ops:
  0.6 0.7 %copy-start.2 = (s32[4,8]{1,0:T(4,128)S(1)}, s32[4,8]{1,0:T(4,128)}, u32[]{:S(2)}) copy-start(s32[4,8]{1,0:T(4,128)} %slots_ref.5) | copy-start | bytes 388
  0.6 0.7 %copy-start.4 = (f32[128]{0:T(128)S(1)}, f32[128]{0:T(128)}, u32[]{:S(2)}) copy-start(f32[128]{0:T(128)} %param.20) | copy-start | bytes 1540
  0.7 0.7 %copy-start.5 = (s32[32]{0:T(128)S(1)}, s32[32]{0:T(128)}, u32[]{:S(2)}) copy-start(s32[32]{0:T(128)} %active_ref.1) | copy-start | bytes 388
  0.7 0.7 %copy-start.6 = (f32[32]{0:T(128)S(1)}, f32[32]{0:T(128)}, u32[]{:S(2)}) copy-start(f32[32]{0:T(128)} %mix_ref.1) | copy-start | bytes 388
  1.3 1.2 %copy-start = (bf16[6,72,1024]{2,1,0:T(8,128)(2,1)S(1)}, bf16[6,72,1024]{2,1,0:T(8,128)(2,1)}, u32[]{:S(2)}) copy-start(bf16[6,72,1024]{2,1,0:T(8,128)(2,1)} %state_ref.1) | copy-start | bytes 2654212
  2.5 0.7 %copy-start.3 = (s32[4,8]{1,0:T(4,128)S(1)}, s32[4,8]{1,0:T(4,128)}, u32[]{:S(2)}) copy-start(s32[4,8]{1,0:T(4,128)} %codes_ref.5) | copy-start | bytes 388
  3.2 0.7 %copy-start.7 = (f32[32]{0:T(128)S(1)}, f32[32]{0:T(128)}, u32[]{:S(2)}) copy-start(f32[32]{0:T(128)} %drift_ref.1) | copy-start | bytes 388
  3.8 0.7 %copy-start.8 = (f32[32]{0:T(128)S(1)}, f32[32]{0:T(128)}, u32[]{:S(2)}) copy-start(f32[32]{0:T(128)} %cond_ref.1) | copy-start | bytes 388
  4.5 0.7 %copy-start.9 = (f32[72]{0:T(128)S(1)}, f32[72]{0:T(128)}, u32[]{:S(2)}) copy-start(f32[72]{0:T(128)} %param.19) | copy-start | bytes 868
  5.2 7.1 %copy-start.1 = (f32[224,128]{1,0:T(8,128)S(1)}, f32[224,128]{1,0:T(8,128)}, u32[]{:S(2)}) copy-start(f32[224,128]{1,0:T(8,128)} %constant.7.clone.table_ref) | copy-start | bytes 344068
  11.7 1.5 %collective-permute-start.2 = (f32[56,512]{1,0:T(8,128)S(1)}, f32[56,512]{1,0:T(8,128)S(1)}, u32[]{:S(2)}, u32[]{:S(2)}) collective-permute-start(f32[56,512]{1,0:T(8,128)S(1)} %get-tuple-element.58.own_ref), channel_id=1, source_target_pairs={{0,16},{16,0},{1,17},{17,1},{2,18},{18,2},{3,19},{19,3},{4,20},{20... | collective-permute-start | bytes 344072 | tf_op jit(solution)/shard_map/ppermute | solution.py:534
  13.4 9.9 %collective-permute-start.3 = (f32[32,512]{1,0:T(8,128)S(1)}, f32[32,512]{1,0:T(8,128)S(1)}, u32[]{:S(2)}, u32[]{:S(2)}) collective-permute-start(f32[32,512]{1,0:T(8,128)S(1)} %get-tuple-element.59), channel_id=1, source_target_pairs={{0,1},{1,0},{2,3},{3,2},{4,5},{5,4},{6,7},{7,6},{8,9},{9,8},{10,11... | collective-permute-start | bytes 196616 | tf_op jit(solution)/shard_map/ppermute | solution.py:529
  16.3 7.9 %collective-permute-start.4 = (f32[32,512]{1,0:T(8,128)S(1)}, f32[32,512]{1,0:T(8,128)S(1)}, u32[]{:S(2)}, u32[]{:S(2)}) collective-permute-start(f32[32,512]{1,0:T(8,128)S(1)} %get-tuple-element.60), channel_id=1, source_target_pairs={{0,15},{1,2},{2,1},{3,4},{4,3},{5,6},{6,5},{7,8},{8,7},{9,10},{10,... | collective-permute-start | bytes 196616 | tf_op jit(solution)/shard_map/ppermute | solution.py:529
  26.5 0.7 %copy-start.10 = (f32[6,72,128]{2,1,0:T(8,128)}, f32[6,72,128]{2,1,0:T(8,128)S(1)}, u32[]{:S(2)}) copy-start(f32[6,72,128]{2,1,0:T(8,128)S(1)} %get-tuple-element.56) | copy-start | bytes 663556

commit v2 on v1

--- a/solution.py
+++ b/solution.py
@@ -200,147 +200,207 @@
     return tables[start : start + 4 * size.edges, :]
 
 
-def crm_kernel(
-    size,
-    levels,
-    width,
-    state_ref,
-    active_ref,
-    mix_ref,
-    drift_ref,
-    cond_ref,
-    mixz_ref,
-    slots_ref,
-    codes_ref,
-    mass_ref,
-    new_ref,
-    face_ref,
-    in_buf,
-    out_buf,
-    in_sem,
-    out_sem,
-):
-    fields = in_buf.shape[1]
+SUBLANES = 8
+
+
+def crm_kernel(size, levels, width, count, *refs):
+    state_hbm, given = refs[0], refs[1 : 1 + count]
+    new_ref, face_ref = refs[1 + count : 3 + count]
+    held = refs[3 + count : 3 + 2 * count]
+    state_ref, table_ref, wide_ref, out_buf, base_ref, inc_ref, state_sem, held_sem = refs[
+        3 + 2 * count :
+    ]
+    fields = state_ref.shape[0]
+    steps = levels // SUBLANES
     per_lane = LANES // width
-
-    def load(e):
+    full = (SUBLANES, LANES)
+    lane = iota(full, 1)
+    pair_lanes = 2 * LANES
+    pairs = size.elements // 2
+
+    def load(p):
+        lanes = pl.ds(pl.multiple_of(p * pair_lanes, pair_lanes), pair_lanes)
         return pltpu.make_async_copy(
-            state_ref.at[:, :, pl.ds(e * LANES, LANES)], in_buf.at[e], in_sem.at[e]
+            state_hbm.at[:, :, lanes], state_ref.at[:, :, lanes], state_sem.at[p]
         )
 
-    def save(e):
-        return pltpu.make_async_copy(
-            out_buf.at[e], new_ref.at[:, :, pl.ds(e * LANES, LANES)], out_sem.at[e]
-        )
-
-    for e in range(size.elements):
-        load(e).start()
-
-    eye = iota((levels, levels), 0) == iota((levels, levels), 1)
-    mixz = jnp.broadcast_to(mixz_ref[...], (levels, levels))
+    small = [
+        pltpu.make_async_copy(src, dst, held_sem.at[n])
+        for n, (src, dst) in enumerate(zip(given, held))
+    ]
+    for copy in small:
+        copy.start()
+    for p in range(pairs):
+        load(p).start()
+    table_ref[...] = jnp.zeros(table_ref.shape, F32)
+    base_ref[...] = jnp.zeros(base_ref.shape, F32)
+    inc_ref[...] = jnp.zeros(inc_ref.shape, F32)
+    for copy in small:
+        copy.wait()
+    first = 0
+    for ref in held:
+        rows, lanes = ref.shape
+        table_ref[first : first + rows, 0:lanes] = ref[...].astype(F32)
+        first += rows
+    params = table_ref[...]
+
+    def spread(ref, i):
+        return ref[pl.ds(i, SUBLANES, stride=steps), :]
+
+    eye = iota((levels, LANES), 0) == iota((levels, LANES), 1)
+    mixz = jnp.broadcast_to(params[4:5, :], (levels, LANES))
     couple = jnp.sum(jnp.where(eye, mixz, 0.0), axis=1, keepdims=True)
     couple = jnp.where(iota((levels, 1), 0) < levels - 1, couple, 0.0)
-    couple = jnp.broadcast_to(couple, (levels, LANES))
-    level = iota((levels, LANES), 0)
-    lane = iota((1, LANES), 1)
-    group = lane // width
-    at_last = jnp.broadcast_to(lane % width == width - 1, (levels, LANES))
-    at_first = jnp.broadcast_to(lane % width == 0, (levels, LANES))
-
-    def lanes_of(ref, e):
-        row = jnp.full((1, LANES), ref[e * per_lane], ref.dtype)
-        for c in range(1, per_lane):
-            row = jnp.where(group == c, ref[e * per_lane + c], row)
-        return row
-
-    def element(e):
-        load(e).wait()
-        mix = lanes_of(mix_ref, e)
-        half = 0.5 * lanes_of(drift_ref, e)
-        rate = jnp.broadcast_to(lanes_of(cond_ref, e), (levels, LANES))
-        alive = level < lanes_of(active_ref, e)
-        centre = jnp.broadcast_to(1.0 - 2.0 * mix, (levels, LANES))
-        east_c = jnp.broadcast_to(mix - half, (levels, LANES))
-        west_c = jnp.broadcast_to(mix + half, (levels, LANES))
+    wide_ref[0, 0] = jnp.broadcast_to(couple, (levels, LANES))
+    coupling = [spread(wide_ref.at[0, 0], i) for i in range(steps)]
+
+    def vertical(a):
+        above = a[1:] + [pltpu.roll(a[0], SUBLANES - 1, 0)]
+        flux = [c * (u - v) for c, u, v in zip(coupling, above, a)]
+        below = [pltpu.roll(flux[-1], 1, 0)] + flux[:-1]
+        return [v + f - b for v, f, b in zip(a, flux, below)]
+
+    level = [iota(full, 0) * steps + i for i in range(steps)]
+    first = lane - lane % width
+    east_lane = first + (lane + 1) % width
+    west_lane = first + (lane + width - 1) % width
+
+    def lanes_of(value, index):
+        return jnp.take_along_axis(value, index, axis=1)
+
+    def element(e, half):
+        here = lanes_of(params[0:SUBLANES, :], e * per_lane + lane // width)
+
+        def row(r):
+            return jnp.broadcast_to(here[r : r + 1, :], full)
+
+        active, mix, drift, rate = row(0).astype(I32), row(1), row(2), row(3)
+        centre, east_c, west_c = 1.0 - 2.0 * mix, mix - 0.5 * drift, mix + 0.5 * drift
+        alive = [v < active for v in level]
+        ice = [jnp.where(v, 0.15, 0.0) for v in alive]
+        lanes = pl.ds(pl.multiple_of(e * LANES, LANES), LANES)
 
         def transport(a):
-            east = jnp.where(
-                at_last, pltpu.roll(a, width - 1, 1), pltpu.roll(a, LANES - 1, 1)
-            )
-            west = jnp.where(
-                at_first, pltpu.roll(a, LANES - width + 1, 1), pltpu.roll(a, 1, 1)
-            )
-            a = centre * a + east_c * east + west_c * west
-            flux = couple * (pltpu.roll(a, levels - 1, 0) - a)
-            return a + flux - pltpu.roll(flux, 1, 0)
-
-        start = [in_buf[e, f].astype(F32) for f in range(fields)]
-        cur = list(start)
+            a = [
+                centre * v + east_c * lanes_of(v, east_lane) + west_c * lanes_of(v, west_lane)
+                for v in a
+            ]
+            return vertical(a)
+
+        cur = []
+        for f in range(fields):
+            wide_ref[half, f] = state_ref[f, :, lanes].astype(F32)
+            cur.append([spread(wide_ref.at[half, f], i) for i in range(steps)])
+        changes = []
         for substep in range(NSUB):
             cur = [transport(a) for a in cur]
-            t, qv, ql, qi = cur[:4]
-            sat = 0.5 * jnp.exp(0.3 * t)
-            cond = jnp.where(alive, jnp.maximum(rate * (qv - sat), -ql), 0.0)
-            qv = qv - cond
-            ql = ql + cond
-            t = t + 0.5 * cond
-            freeze = jnp.where(alive, 0.15 * ql * (1.0 - jnp.tanh(t)), 0.0)
-            ql = ql - freeze
-            qi = qi + freeze
-            t = t + 0.1 * freeze
-            cur[:4] = [t, qv, ql, qi]
+            conds, freezes = [], []
+            for i in range(steps):
+                t, qv, ql, qi = [cur[f][i] for f in range(4)]
+                sat = jnp.exp2((0.3 * math.log2(math.e)) * t - 1.0)
+                cond = jnp.where(alive[i], jnp.maximum(rate * (qv - sat), -ql), 0.0)
+                ql = ql + cond
+                t = t + 0.5 * cond
+                freeze = ice[i] * ql * (1.0 - jnp.tanh(t))
+                cur[0][i] = t + 0.1 * freeze
+                cur[1][i] = qv - cond
+                cur[2][i] = ql - freeze
+                cur[3][i] = qi + freeze
+                conds.append(cond)
+                freezes.append(freeze)
+            changes += conds + freezes
         for f in range(fields):
-            out_buf[e, f] = cur[f].astype(BF16)
-        save(e).start()
-        return jnp.concatenate([cur[f] - start[f] for f in range(fields)], axis=0)
-
-    pair_lanes = 2 * LANES
-    cell_of = iota((2 * per_lane, pair_lanes), 1) // width
-    mean = jnp.where(iota((2 * per_lane, pair_lanes), 0) == cell_of, PER_TIME / width, 0.0)
-    mean = mean.astype(BF16)
-    face_ref[...] = jnp.zeros(face_ref.shape, F32)
-
-    def pair(i, carry):
-        diff = jnp.concatenate([element(2 * i), element(2 * i + 1)], axis=1)
-        high = diff.astype(BF16)
-        low = (diff - high.astype(F32)).astype(BF16)
-        rows = dot_nt(mean, high, None) + dot_nt(mean, low, None)
-        face_ref[pl.ds(pl.multiple_of(i * 2 * per_lane, 8), 2 * per_lane), 0 : size.flat] = rows
+            for i in range(steps):
+                out_buf[half, f, pl.ds(i, SUBLANES, stride=steps), :] = cur[f][i]
+            new_ref[f, :, lanes] = out_buf[half, f].astype(BF16)
+        return jnp.concatenate(changes, axis=0)
+
+    cells = pair_lanes // width
+    group = iota((pair_lanes, LANES), 0) // width == iota((pair_lanes, LANES), 1) % cells
+    total = jnp.where(group, 1.0, 0.0).astype(BF16)
+
+    def pair(p, carry):
+        load(p).wait()
+        mine = lane // cells == p
+        lanes = pl.ds(pl.multiple_of(p * pair_lanes, pair_lanes), pair_lanes)
+        for f in range(fields):
+            sums = dot_nn(state_ref[f, :, lanes], total, None)
+            keep = jnp.broadcast_to(mine[0:1, :], sums.shape)
+            base_ref[f] = jnp.where(keep, sums, base_ref[f])
+        change = jnp.concatenate([element(2 * p, 0), element(2 * p + 1, 1)], axis=1)
+        high = change.astype(BF16)
+        low = (change - high.astype(F32)).astype(BF16)
+        sums = dot_nn(high, total, None) + dot_nn(low, total, None)
+        keep = jnp.broadcast_to(mine[0:1, :], sums.shape)
+        inc_ref[...] = jnp.where(keep, sums, inc_ref[...])
         return carry
 
-    lax.fori_loop(0, size.elements // 2, pair, 0)
-
+    lax.fori_loop(0, pairs, pair, 0)
+
+    def change_of(n):
+        return [
+            inc_ref[(n * steps + i) * SUBLANES : (n * steps + i + 1) * SUBLANES, :]
+            for i in range(steps)
+        ]
+
+    parts = [[change_of(2 * n), change_of(2 * n + 1)] for n in range(NSUB)]
     parity = lax.axis_index("tile") % 2
-    slots_row = flat_row(slots_ref[...])
-    codes_row = flat_row(codes_ref[...])
-    edges = Edges(size, slots_row, codes_row, parity)
+    slots_row = flat_row(params[6:10, 0 : size.elements])
+    codes_row = flat_row(params[10:14, 0 : size.elements])
+    edges = Edges(size, slots_row.astype(I32), codes_row.astype(I32), parity)
     slot = side_slots(size, edges.side, edges.flat)
     rows = 2 * size.raw
-    place = jnp.where(edges.side >= 0, edges.side * size.raw + 2 * slot, -8)
+    place = jnp.where(edges.side >= 0, size.cells + edges.side * size.raw + 2 * slot, -8)
     put = jnp.concatenate([place, place + 1], axis=1)
-    select = jnp.where(iota((rows, 2 * size.edges), 0) == put, 1.0, 0.0)
     cell = jnp.concatenate(
         [4 * edges.e + edge_cell(edges.k, m) for m in range(2)], axis=1
     )
-    cell_t = jnp.where(iota((size.cells, 2 * size.edges), 0) == cell, 1.0, 0.0)
-    pick = dot_nt(select, cell_t, None)
-    face_ref[size.cells : size.cells + rows, :] = dot_nn(pick, face_ref[0 : size.cells, :])
+    select = jnp.where(iota((LANES, 2 * size.edges), 0) == put, 1.0, 0.0)
+    cell = jnp.broadcast_to(cell.astype(F32), (SUBLANES, 2 * size.edges))
+    picked = dot_nt(cell, select, None).astype(I32)
+    source = jnp.where(lane < size.cells, lane, picked)
+
+    scale = PER_TIME / width
+    columns = []
+    for f in range(fields):
+        start = [spread(base_ref.at[f], i) for i in range(steps)]
+        mean = start
+        for cond, freeze in parts:
+            mean = vertical(mean)
+            if f == 0:
+                mean = [v + 0.5 * c + 0.1 * z for v, c, z in zip(mean, cond, freeze)]
+            elif f == 1:
+                mean = [v - c for v, c in zip(mean, cond)]
+            elif f == 2:
+                mean = [v + c - z for v, c, z in zip(mean, cond, freeze)]
+            elif f == 3:
+                mean = [v + z for v, z in zip(mean, freeze)]
+        columns += [lanes_of(scale * (v - s), source) for v, s in zip(mean, start)]
+    columns.append(jnp.zeros((size.wide - size.flat, LANES), F32))
+    tendency = jnp.concatenate(columns, axis=0)
     base = size.cells + rows
-    face_ref[base : base + 1, 0 : size.edges] = slots_row.astype(F32)
-    face_ref[base + 1 : base + 2, 0 : size.edges] = codes_row.astype(F32)
-    face_ref[base + 2 : base + 3, 0 : size.points] = mass_ref[...]
-
-    for e in range(size.elements):
-        save(e).wait()
-
-
-def weights_kernel(size, slots_ref, codes_ref, mass_ref, table_ref, part_ref):
+    face_ref[0:base, :] = tendency.T[0:base, :]
+    face_ref[base:, :] = jnp.zeros((SUBLANES, size.wide), F32)
+    face_ref[base : base + 1, 0 : size.edges] = slots_row
+    face_ref[base + 1 : base + 2, 0 : size.edges] = codes_row
+    face_ref[base + 2 : base + 3, 0 : size.points] = params[5:6, 0 : size.points]
+
+
+def face_edges(size, face_ref, parity):
+    base = size.cells + 2 * size.raw
+    slots_row = face_ref[base : base + 1, 0 : size.edges].astype(I32)
+    codes_row = face_ref[base + 1 : base + 2, 0 : size.edges].astype(I32)
+    mass_row = face_ref[base + 2 : base + 3, 0 : size.points]
+    return Edges(size, slots_row, codes_row, parity), mass_row
+
+
+def weights_kernel(size, own_ref, table_ref, part_ref):
     parity = lax.axis_index("tile") % 2
-    edges = Edges(size, flat_row(slots_ref[...]), flat_row(codes_ref[...]), parity)
+    edges, mass_row = face_edges(size, own_ref, parity)
     tables = table_ref[...]
     slot_far = side_slots(size, edges.side, edges.other_flat)
     oper_t = operator_t(
-        size, tables, gather_matrix_t(size, edges, slot_far, 0), mass_ref[...], False
+        size, tables, gather_matrix_t(size, edges, slot_far, 0), mass_row, False
     )
     slot = side_slots(size, edges.side, edges.flat)
     rows = 2 * size.part
@@ -378,33 +438,19 @@
 
 
 def inner_kernel(
-    size,
-    slots_ref,
-    codes_ref,
-    mass_ref,
-    table_ref,
-    own_ref,
-    twin_ref,
-    sum_ref,
-    near_ref,
-    matrix_ref,
+    size, table_ref, own_ref, twin_ref, state_ref, sum_ref, near_ref, matrix_ref, new_ref, sem
 ):
+    save = pltpu.make_async_copy(state_ref, new_ref, sem)
+    save.start()
     parity = lax.axis_index("tile") % 2
     tables = table_ref[...]
-    base = size.cells + 2 * size.raw
-    own = Edges(size, flat_row(slots_ref[...]), flat_row(codes_ref[...]), parity)
-    twin = Edges(
-        size,
-        twin_ref[base : base + 1, 0 : size.edges].astype(I32),
-        twin_ref[base + 1 : base + 2, 0 : size.edges].astype(I32),
-        parity,
-    )
-    twin_mass = twin_ref[base + 2 : base + 3, 0 : size.points]
+    own, own_mass = face_edges(size, own_ref, parity)
+    twin, twin_mass = face_edges(size, twin_ref, parity)
     own_slot = side_slots(size, own.side, own.other_flat)
     twin_slot = side_slots(size, twin.side, twin.other_flat)
     oper = jnp.concatenate(
         [
-            operator_t(size, tables, gather_matrix_t(size, own, own_slot, 0), mass_ref[...], False),
+            operator_t(size, tables, gather_matrix_t(size, own, own_slot, 0), own_mass, False),
             operator_t(size, tables, gather_matrix_t(size, twin, twin_slot, 1), twin_mass, True),
         ],
         axis=1,
@@ -451,10 +497,27 @@
     )
     cell_t = jnp.where(iota((size.cells, 2 * size.edges), 0) == cell, 1.0, 0.0)
     near_ref[...] = dot_nn(dot_nt(weight, cell_t), own_ref[0 : size.cells, :])
-
-
-def final_kernel(size, even_ref, odd_ref, sum_ref, near_ref, matrix_ref, out_ref, keep_ref):
+    save.wait()
+
+
+def final_kernel(
+    size,
+    levels,
+    even_ref,
+    odd_ref,
+    sum_ref,
+    near_ref,
+    matrix_ref,
+    part_ref,
+    out_ref,
+    keep_ref,
+    flag_ref,
+):
     raw = 2 * size.raw
+    mine = part_ref[0:1, size.ops : size.ops + 1]
+    others = [ref[raw : raw + 1, size.flat + 1 : size.flat + 2] for ref in (even_ref, odd_ref)]
+    flag = jnp.where(mine + others[0] + others[1] > 0.0, 1.0, 0.0)
+    flag_ref[0, 0] = jnp.sum(flag).astype(I32)
     mass = jnp.concatenate(
         [ref[raw:, size.flat : size.flat + 1] for ref in (even_ref, odd_ref)], axis=0
     )
@@ -463,20 +526,20 @@
     rows = jnp.concatenate([even_ref[0:raw, :], odd_ref[0:raw, :], part], axis=0)
     n = 2 * raw + 2 * size.part
     side = matrix_ref[2 * raw : n, :]
+    mass_sum = matrix_ref[n : n + 1, :] + jnp.sum(side * mass, axis=0, keepdims=True)
+    keep_ref[...] = jnp.broadcast_to(mass_sum, (8, size.points))
     total = sum_ref[...] + dot_tn(rows[:, 0 : size.flat], matrix_ref[0:n, :])
-    mass_sum = matrix_ref[n : n + 1, :] + jnp.sum(side * mass, axis=0, keepdims=True)
-    out_ref[...] = total / mass_sum
-    keep_ref[0:1, :] = mass_sum
-    row = jnp.concatenate(
-        [ref[raw : raw + 1, size.flat + 1 : size.flat + 2] for ref in (even_ref, odd_ref)], axis=0
-    )
-    keep_ref[1:3, :] = jnp.broadcast_to(row, (2, size.points))
-    keep_ref[3:, :] = jnp.zeros((5, size.points), F32)
+    total = total / mass_sum
+    steps = levels // SUBLANES
+    for f in range(size.flat // levels):
+        for i in range(steps):
+            row = (f * steps + i) * SUBLANES
+            out_ref[pl.ds(f * levels + i, SUBLANES, stride=steps), :] = total[row : row + SUBLANES, :]
 
 
 VMEM = pl.BlockSpec(memory_space=pltpu.VMEM)
 SMEM = pl.BlockSpec(memory_space=pltpu.SMEM)
-ANY = pl.BlockSpec(memory_space=pl.ANY)
+HBM = pl.BlockSpec(memory_space=pltpu.HBM)
 
 
 def call(body, name, outs, ins, in_specs=None, out_specs=None, scratch=(), limit=8):
@@ -495,22 +558,32 @@
     return jax.ShapeDtypeStruct(dims, F32)
 
 
-def advance(size, crm_state, column_args, mix_z, slots, codes, mass_row):
+def advance(size, crm_state, params):
     fields, levels, lanes = crm_state.shape
-    width = lanes // column_args[0].shape[0]
-    buffers = (size.elements, fields, levels, LANES)
+    width = lanes // size.cells
+    block = pltpu.VMEM((2, fields, levels, LANES), F32)
+    params = [value.reshape(-1, value.shape[-1]) for value in params]
+    rows = sum(value.shape[0] for value in params)
+    ins = [pltpu.with_memory_space_constraint(value, pltpu.HBM) for value in (crm_state, *params)]
     return call(
-        functools.partial(crm_kernel, size, levels, width),
+        functools.partial(crm_kernel, size, levels, width, len(params)),
         "advance",
-        [jax.ShapeDtypeStruct(crm_state.shape, BF16), shape_of(size.face_rows, size.wide)],
-        [crm_state, *column_args, mix_z.reshape(1, levels), slots, codes, mass_row],
-        in_specs=[ANY] + [SMEM] * 4 + [VMEM] * 4,
-        out_specs=[ANY, VMEM],
-        scratch=[
-            pltpu.VMEM(buffers, BF16),
-            pltpu.VMEM(buffers, BF16),
-            pltpu.SemaphoreType.DMA((size.elements,)),
-            pltpu.SemaphoreType.DMA((size.elements,)),
+        [
+            pltpu.VMEM(crm_state.shape, BF16),
+            pltpu.VMEM((size.face_rows, size.wide), F32),
+        ],
+        ins,
+        in_specs=[HBM] * len(ins),
+        scratch=[pltpu.VMEM(value.shape, value.dtype) for value in params]
+        + [
+            pltpu.VMEM(crm_state.shape, BF16),
+            pltpu.VMEM((-(-rows // SUBLANES) * SUBLANES, LANES), F32),
+            block,
+            block,
+            pltpu.VMEM((fields, levels, LANES), F32),
+            pltpu.VMEM((2 * NSUB * levels, LANES), F32),
+            pltpu.SemaphoreType.DMA((size.elements // 2,)),
+            pltpu.SemaphoreType.DMA((len(params),)),
         ],
         limit=16,
     )
@@ -534,14 +607,14 @@
     return lax.ppermute(value, axis, [(s, (s + steps) % count) for s in range(count)])
 
 
-def assemble_pair(size, face, slots, codes, mass_row):
+def assemble_pair(size, levels, state, face):
     tables = jnp.asarray(constant_tables(size))
     twin = shift(face, "face", 1)
     (part,) = call(
         functools.partial(weights_kernel, size),
         "weights",
         [shape_of(2 * size.part, LANES)],
-        [slots, codes, mass_row, tables],
+        [face, tables],
     )
     message = shape_of(size.tile_rows, size.wide)
     even, odd = call(
@@ -550,43 +623,107 @@
     odd_in = swap(odd, True)
     even_in = swap(even, False)
     extra = 4 * size.raw + 2 * size.part
-    inner, near, matrix = call(
+    inner, near, matrix, new_state = call(
         functools.partial(inner_kernel, size),
         "inner",
         [
             shape_of(size.flat, size.points),
             shape_of(2 * size.part, size.wide),
             shape_of(extra + 8, size.points),
+            pltpu.HBM(state.shape, state.dtype),
         ],
-        [slots, codes, mass_row, tables, face, twin],
-    )
-    out, keep = call(
-        functools.partial(final_kernel, size),
+        [tables, face, twin, pltpu.with_memory_space_constraint(state, pltpu.VMEM)],
+        out_specs=[VMEM, VMEM, VMEM, HBM],
+        scratch=[pltpu.SemaphoreType.DMA],
+    )
+    out, keep, flag = call(
+        functools.partial(final_kernel, size, levels),
         "final",
-        [shape_of(size.flat, size.points), shape_of(8, size.points)],
-        [even_in, odd_in, inner, near, matrix],
-    )
-    return out, part, keep, matrix, even_in, odd_in
-
-
-def second_exchange(size, out, part, keep, matrix, even_in, odd_in):
+        [
+            pltpu.VMEM((size.flat, size.points), F32),
+            shape_of(8, size.points),
+            pltpu.SMEM((1, 1), I32),
+        ],
+        [even_in, odd_in, inner, near, matrix, part],
+        out_specs=[VMEM, VMEM, SMEM],
+    )
+    return new_state, (out, part, keep, matrix, even_in, odd_in, flag)
+
+
+def one_of(index, branches, *operands):
+    whole = jax.make_jaxpr(lambda i, *rest: lax.switch(i, branches, *rest))(index, *operands)
+    last = whole.jaxpr.eqns[-1]
+    return last.primitive.bind(index, *operands, **last.params)[0]
+
+
+def second_exchange(size, levels, out, part, keep, matrix, even_in, odd_in, flag):
     raw = 2 * size.raw
-    mine = part[0, size.ops] > 0.0
-    inputs = (even_in, odd_in)
-    for s in range(2):
-        source = inputs[1 - s]
+
+    def add(s, value, part, keep, matrix, even_in, odd_in):
+        source = (odd_in, even_in)[s]
         first = 2 * size.cells + raw * (1 - s)
         weights = part[s * size.part : (s + 1) * size.part, first : first + raw]
         side = matrix[2 * raw + s * size.part : 2 * raw + (s + 1) * size.part, :]
-        wanted = jnp.logical_or(mine, keep[1 + s, 0] > 0.0)
-
-        def add(value, s=s, source=source, weights=weights, side=side):
-            sent = jnp.dot(weights, source[0:raw, 0 : size.flat], precision=HI)
-            got = swap(sent, s == 1)
-            return value + jnp.dot(got.T, side, precision=HI) / keep[0:1, :]
-
-        out = lax.cond(wanted, add, lambda value: value, out)
-    return out
+        sent = jnp.dot(weights, source[0:raw, 0 : size.flat], precision=HI)
+        got = swap(sent, s == 1)
+        more = jnp.dot(got.T, side, precision=HI) / keep[0:1, :]
+        more = more.reshape(-1, levels // SUBLANES, SUBLANES, size.points)
+        return value + more.transpose(0, 2, 1, 3).reshape(value.shape)
+
+    def none(value, *rest):
+        return value
+
+    def some(value, *rest):
+        mine = rest[0][0, size.ops]
+        for s, received in ((0, rest[3]), (1, rest[4])):
+            other = received[raw, size.flat + 1]
+            value = lax.cond(
+                mine + other > 0.0, functools.partial(add, s), none, value, *rest
+            )
+        return value
+
+    operands = (out, part, keep, matrix, even_in, odd_in)
+    return one_of(flag[0, 0], (none, some), *operands)
+
+
+def oriented(edge_lists):
+    rows = []
+    for code in range(8):
+        side = list(edge_lists[code // 2])
+        rows.append(side[::-1] if code % 2 == 1 else side)
+    return np.array(rows, np.int32)
+
+
+def collect(value, slots):
+    pieces = [value]
+    for axis, steps in (("tile", 1), ("tile", -1), ("face", 1), ("face", -1)):
+        pieces.append(shift(value, axis, steps))
+    return jnp.concatenate(pieces, axis=0), slots
+
+
+def assemble_any(size, levels, face, masses, slots, codes):
+    elements = size.elements
+    cells = face[0 : size.cells, 0 : size.flat].reshape(elements, 4, size.flat)
+    pool, rows = collect(cells, slots)
+    pick = jnp.take(jnp.asarray(oriented(CELL_EDGE)), codes, axis=0)
+    index = (rows[:, :, None] * 4 + pick).transpose(1, 0, 2).reshape(-1)
+    across = jnp.take(pool.reshape(-1, size.flat), index, axis=0)
+    stacked = jnp.concatenate([cells, across.reshape(elements, 8, size.flat)], axis=1)
+    points = jnp.einsum("ecz,pc->epz", stacked, jnp.asarray(remap_matrix()), precision=HI)
+    masses = masses.reshape(elements, 16)
+    numerator, denominator = points * masses[:, :, None], masses
+    weighted, rows = collect(numerator, slots)
+    mass_pool, _ = collect(masses, slots)
+    pick = jnp.take(jnp.asarray(oriented(GLL_EDGE)), codes, axis=0)
+    for k in range(4):
+        index = (rows[k][:, None] * 16 + pick[k]).reshape(-1)
+        got = jnp.take(weighted.reshape(-1, size.flat), index, axis=0)
+        numerator = numerator.at[:, GLL_EDGE[k]].add(got.reshape(elements, 4, size.flat))
+        got = jnp.take(mass_pool.reshape(-1), index)
+        denominator = denominator.at[:, GLL_EDGE[k]].add(got.reshape(elements, 4))
+    ratio = (numerator / denominator[:, :, None]).reshape(size.points, size.flat)
+    ratio = ratio.reshape(size.points, -1, levels // SUBLANES, SUBLANES)
+    return ratio.transpose(1, 3, 2, 0).reshape(size.flat, size.points)
 
 
 def local(
@@ -602,18 +739,24 @@
 ):
     fields, levels, _ = crm_state.shape
     size = Sizes(neighbor_slots.shape[1], fields * levels)
-    mass_row = point_mass.reshape(1, size.points)
-    new_state, face = advance(
-        size,
-        crm_state,
-        (active_levels, mix_x, drift_speed, cond_rate),
+    params = (
+        active_levels,
+        mix_x,
+        drift_speed,
+        cond_rate,
         mix_z,
+        point_mass,
         neighbor_slots,
         edge_codes,
-        mass_row,
-    )
-    results = assemble_pair(size, face, neighbor_slots, edge_codes, mass_row)
-    out = second_exchange(size, *results)
+    )
+    state, face = advance(size, crm_state, params)
+    tiles = lax.axis_size("tile")
+    if lax.axis_size("face") == 2 and tiles % 2 == 0 and tiles > 2:
+        new_state, results = assemble_pair(size, levels, state, face)
+        out = second_exchange(size, levels, *results)
+    else:
+        new_state = state
+        out = assemble_any(size, levels, face, point_mass, neighbor_slots, edge_codes)
     return (new_state, out.reshape(fields, levels, size.points))
 
 

time: 27.4 us -> 20.2 us (0.74)
  local copies, waits for them, and re-layouts: 6.28 us -> 0.71 us
  between operations: 2.67 us -> 0.7 us
  waiting for transfers between devices: 1.24 us -> 2.51 us
  Pallas kernels: 9.01 us -> 8.08 us
    unnamed x22 -> x4, local copies, waits for them, and re-layouts: 5.17 us -> 0.71 us
    ppermute x2, waiting for transfers between devices: 0.87 us -> 2.14 us  [swap(): return lax.ppermute(value, 'tile', swap_pairs(odd))]
    slice x2 -> x0, local copies, waits for them, and re-layouts: 1.11 us -> none  [the longest x1 0.58 us: second_exchange(): mine = part[0, size.ops] > 0.0]
    pallas_call x5, Pallas kernels: 9.01 us -> 8.08 us  [call(): pl.pallas_call(body, out_shape=outs, in_specs=in_specs or [VMEM] * len(in...]
  transfers between devices with their start and end apart: 3 -> 3, of which waited for: 2 -> 2; matrix products, arithmetic and copies ran while one was open for 2% -> 0% of each run, Pallas kernels for 7% -> 9%
where the time goes in v2:
time: 20.2 us; the launch traced here: 20 us
  Pallas kernels  8.08 us (40%)
  starting transfers between devices  7.98 us (40%)
  waiting for transfers between devices  2.51 us (12%)
  local copies, waits for them, and re-layouts  0.71 us (4%)
  between operations  0.7 us (3%)
    pallas_call x5, Pallas kernels, call(): pl.pallas_call(body, out_shape=outs, in_specs=in_specs or [VMEM] * len(in...  8.08 us
    ppermute x2, starting transfers between devices, swap(): return lax.ppermute(value, 'tile', swap_pairs(odd))  7.43 us
    ppermute x2, waiting for transfers between devices, swap(): return lax.ppermute(value, 'tile', swap_pairs(odd))  2.14 us
    unnamed x4, local copies, waits for them, and re-layouts  0.71 us
    ppermute x1, starting transfers between devices, shift(): lax.ppermute(value, axis, [(s, (s + steps) % count) for s in range(count)])  0.56 us
  transfers between devices with their start and end apart: 3, of which 2 were waited for; matrix products, arithmetic and copies ran while one was open for 0% of the time, Pallas kernels for 9%

profile of v2, /device:TPU:0, one launch (start us, length us, event | category | flops | bytes accessed | tf_op | source)
XLA Modules:
  0.0 20.0 jit_solution(5180962148154955067)
XLA Ops:
  0.6 0.0 copy-start
  0.6 5.7 %advance.1 = (bf16[6,72,1024]{2,1,0:T(8,128)(2,1)S(1)}, f32[56,512]{1,0:T(8,128)S(1)}) custom-call(bf16[6,72,1024]{2,1,0:T(8,128)(2,1)} %refs_0_.1, s32[1,32]{1,0:T(1,128)} %bitcast.31, f32[1,32]{1,0:T(1,128)} %bitcast.32, f32[1,32]{1,0:T(1,128)} %bitcast.33, f32[1,32]{1,0:T(1,128)} %bitcast.34, f32[1,72]{1,0:T(1,128)} %bitcast.35, f32[1,128]{1,0:T(1,128)} %bitcast.36, ...), custom_call_target="tpu_custom_call" | custom-call | tf_op jit(solution)/shard_map/advance/pallas_call | solution.py:546
  6.3 0.6 %collective-permute-start.2 = (f32[56,512]{1,0:T(8,128)S(1)}, f32[56,512]{1,0:T(8,128)S(1)}, u32[]{:S(2)}, u32[]{:S(2)}) collective-permute-start(f32[56,512]{1,0:T(8,128)S(1)} %get-tuple-element.81.own_ref), channel_id=1, source_target_pairs={{0,16},{16,0},{1,17},{17,1},{2,18},{18,2},{3,19},{19,3},{4,20},{20... | collective-permute-start | bytes 344072 | tf_op jit(solution)/shard_map/ppermute | solution.py:607
  6.9 0.0 copy-done
  6.9 0.6 %weights.1.part_ref = f32[32,128]{1,0:T(8,128)S(1)} custom-call(f32[56,512]{1,0:T(8,128)S(1)} %get-tuple-element.81.own_ref, f32[224,128]{1,0:T(8,128)S(1)} %copy-done), custom_call_target="tpu_custom_call" | custom-call | tf_op jit(solution)/shard_map/weights/pallas_call | solution.py:546
  7.5 0.4 %collective-permute-done.2.twin_ref = f32[56,512]{1,0:T(8,128)S(1)} collective-permute-done((f32[56,512]{1,0:T(8,128)S(1)}, f32[56,512]{1,0:T(8,128)S(1)}, u32[]{:S(2)}, u32[]{:S(2)}) %collective-permute-start.2) | collective-permute-done | bytes 114720 | tf_op jit(solution)/shard_map/ppermute | solution.py:607
  7.9 0.2 message.1
  8.1 2.9 %collective-permute-start.3 = (f32[32,512]{1,0:T(8,128)S(1)}, f32[32,512]{1,0:T(8,128)S(1)}, u32[]{:S(2)}, u32[]{:S(2)}) collective-permute-start(f32[32,512]{1,0:T(8,128)S(1)} %get-tuple-element.84), channel_id=1, source_target_pairs={{0,1},{1,0},{2,3},{3,2},{4,5},{5,4},{6,7},{7,6},{8,9},{9,8},{10,11... | collective-permute-start | bytes 196616 | tf_op jit(solution)/shard_map/ppermute | solution.py:602
  11.0 4.5 %collective-permute-start.4 = (f32[32,512]{1,0:T(8,128)S(1)}, f32[32,512]{1,0:T(8,128)S(1)}, u32[]{:S(2)}, u32[]{:S(2)}) collective-permute-start(f32[32,512]{1,0:T(8,128)S(1)} %get-tuple-element.85), channel_id=1, source_target_pairs={{0,15},{1,2},{2,1},{3,4},{4,3},{5,6},{6,5},{7,8},{8,7},{9,10},{10,... | collective-permute-start | bytes 196616 | tf_op jit(solution)/shard_map/ppermute | solution.py:602
  15.5 1.2 %inner.1 = (f32[432,128]{1,0:T(8,128)S(1)}, f32[32,512]{1,0:T(8,128)S(1)}, f32[72,128]{1,0:T(8,128)S(1)}, bf16[6,72,1024]{2,1,0:T(8,128)(2,1)}) custom-call(f32[224,128]{1,0:T(8,128)S(1)} %copy-done, f32[56,512]{1,0:T(8,128)S(1)} %get-tuple-element.81.own_ref, f32[56,512]{1,0:T(8,128)S(1)} %collective-permute-done.2.twin_ref, ...), custom_call_target="tpu_custom_call" | custom-call | tf_op jit(solution)/shard_map/inner/pallas_call | solution.py:546
  16.7 0.0 collective-permute-done.3.even_ref
  16.7 2.1 %collective-permute-done.4.odd_ref = f32[32,512]{1,0:T(8,128)S(1)} collective-permute-done((f32[32,512]{1,0:T(8,128)S(1)}, f32[32,512]{1,0:T(8,128)S(1)}, u32[]{:S(2)}, u32[]{:S(2)}) %collective-permute-start.4) | collective-permute-done | bytes 65568 | tf_op jit(solution)/shard_map/ppermute | solution.py:602
  18.8 0.4 %final.1 = (f32[432,128]{1,0:T(8,128)S(1)}, f32[8,128]{1,0:T(8,128)S(1)}, s32[1,1]{1,0:T(1,128)S(4)}) custom-call(f32[32,512]{1,0:T(8,128)S(1)} %collective-permute-done.3.even_ref, f32[32,512]{1,0:T(8,128)S(1)} %collective-permute-done.4.odd_ref, f32[432,128]{1,0:T(8,128)S(1)} %get-tuple-element.86.sum_ref, f32[32,512]{1,0:T(8,128)S(1)} %get-tuple-element.87.near_ref, ...), custom_call_target="tpu_custom_call" | custom-call | tf_op jit(solution)/shard_map/final/pallas_call | solution.py:546
  19.3 0.7 %copy.28 = f32[6,72,128]{2,1,0:T(8,128)} copy(f32[6,72,128]{2,1,0:T(8,128)S(1)} %get-tuple-element.102) | data formatting | bytes 442368
  (2 shorter events, 0.0 us)
Async XLA Ops:
  0.6 6.3 %copy-start = (f32[224,128]{1,0:T(8,128)S(1)}, f32[224,128]{1,0:T(8,128)}, u32[]{:S(2)}) copy-start(f32[224,128]{1,0:T(8,128)} %constant.6.clone.table_ref) | copy-start | bytes 344068
  6.3 1.5 %collective-permute-start.2 = (f32[56,512]{1,0:T(8,128)S(1)}, f32[56,512]{1,0:T(8,128)S(1)}, u32[]{:S(2)}, u32[]{:S(2)}) collective-permute-start(f32[56,512]{1,0:T(8,128)S(1)} %get-tuple-element.81.own_ref), channel_id=1, source_target_pairs={{0,16},{16,0},{1,17},{17,1},{2,18},{18,2},{3,19},{19,3},{4,20},{20... | collective-permute-start | bytes 344072 | tf_op jit(solution)/shard_map/ppermute | solution.py:607
  8.1 8.6 %collective-permute-start.3 = (f32[32,512]{1,0:T(8,128)S(1)}, f32[32,512]{1,0:T(8,128)S(1)}, u32[]{:S(2)}, u32[]{:S(2)}) collective-permute-start(f32[32,512]{1,0:T(8,128)S(1)} %get-tuple-element.84), channel_id=1, source_target_pairs={{0,1},{1,0},{2,3},{3,2},{4,5},{5,4},{6,7},{7,6},{8,9},{9,8},{10,11... | collective-permute-start | bytes 196616 | tf_op jit(solution)/shard_map/ppermute | solution.py:602
  11.0 7.9 %collective-permute-start.4 = (f32[32,512]{1,0:T(8,128)S(1)}, f32[32,512]{1,0:T(8,128)S(1)}, u32[]{:S(2)}, u32[]{:S(2)}) collective-permute-start(f32[32,512]{1,0:T(8,128)S(1)} %get-tuple-element.85), channel_id=1, source_target_pairs={{0,15},{1,2},{2,1},{3,4},{4,3},{5,6},{6,5},{7,8},{8,7},{9,10},{10,... | collective-permute-start | bytes 196616 | tf_op jit(solution)/shard_map/ppermute | solution.py:602

commit v3 on v2

--- a/solution.py
+++ b/solution.py
@@ -121,6 +121,21 @@
     )
 
 
+def split(value):
+    high = value.astype(BF16)
+    return high, (value - high.astype(F32)).astype(BF16)
+
+
+def stack_left(value, axis):
+    high, low = split(value)
+    return jnp.concatenate([high, low, high], axis=axis)
+
+
+def stack_right(value, axis):
+    high, low = split(value)
+    return jnp.concatenate([high, high, low], axis=axis)
+
+
 def flat_row(table):
     return jnp.concatenate([table[k : k + 1, :] for k in range(4)], axis=1)
 
@@ -207,9 +222,10 @@
     state_hbm, given = refs[0], refs[1 : 1 + count]
     new_ref, face_ref = refs[1 + count : 3 + count]
     held = refs[3 + count : 3 + 2 * count]
-    state_ref, table_ref, wide_ref, out_buf, base_ref, inc_ref, state_sem, held_sem = refs[
-        3 + 2 * count :
+    state_ref, table_ref, wide_ref, out_buf, base_ref, inc_ref, change_ref = refs[
+        3 + 2 * count : 10 + 2 * count
     ]
+    state_sem, held_sem = refs[10 + 2 * count :]
     fields = state_ref.shape[0]
     steps = levels // SUBLANES
     per_lane = LANES // width
@@ -218,11 +234,8 @@
     pair_lanes = 2 * LANES
     pairs = size.elements // 2
 
-    def load(p):
-        lanes = pl.ds(pl.multiple_of(p * pair_lanes, pair_lanes), pair_lanes)
-        return pltpu.make_async_copy(
-            state_hbm.at[:, :, lanes], state_ref.at[:, :, lanes], state_sem.at[p]
-        )
+    def load(f):
+        return pltpu.make_async_copy(state_hbm.at[f], state_ref.at[f], state_sem.at[f])
 
     small = [
         pltpu.make_async_copy(src, dst, held_sem.at[n])
@@ -230,9 +243,10 @@
     ]
     for copy in small:
         copy.start()
-    for p in range(pairs):
-        load(p).start()
+    for f in range(fields):
+        load(f).start()
     table_ref[...] = jnp.zeros(table_ref.shape, F32)
+    change_ref[...] = jnp.zeros(change_ref.shape, F32)
     base_ref[...] = jnp.zeros(base_ref.shape, F32)
     inc_ref[...] = jnp.zeros(inc_ref.shape, F32)
     for copy in small:
@@ -268,7 +282,14 @@
     def lanes_of(value, index):
         return jnp.take_along_axis(value, index, axis=1)
 
-    def element(e, half):
+    def lanes_at(e, count=1):
+        return pl.ds(pl.multiple_of(e * LANES, LANES), count * LANES)
+
+    def widen(e, half):
+        for f in range(fields):
+            wide_ref[half, f] = state_ref[f, :, lanes_at(e)].astype(F32)
+
+    def advance_element(e, half):
         here = lanes_of(params[0:SUBLANES, :], e * per_lane + lane // width)
 
         def row(r):
@@ -278,7 +299,6 @@
         centre, east_c, west_c = 1.0 - 2.0 * mix, mix - 0.5 * drift, mix + 0.5 * drift
         alive = [v < active for v in level]
         ice = [jnp.where(v, 0.15, 0.0) for v in alive]
-        lanes = pl.ds(pl.multiple_of(e * LANES, LANES), LANES)
 
         def transport(a):
             a = [
@@ -287,13 +307,18 @@
             ]
             return vertical(a)
 
-        cur = []
-        for f in range(fields):
-            wide_ref[half, f] = state_ref[f, :, lanes].astype(F32)
-            cur.append([spread(wide_ref.at[half, f], i) for i in range(steps)])
+        def keep(f):
+            for i in range(steps):
+                out_buf[half, f, pl.ds(i, SUBLANES, stride=steps), :] = cur[f][i]
+            new_ref[f, :, lanes_at(e)] = out_buf[half, f].astype(BF16)
+
+        cur = [[spread(wide_ref.at[half, f], i) for i in range(steps)] for f in range(fields)]
         changes = []
         for substep in range(NSUB):
             cur = [transport(a) for a in cur]
+            if substep == NSUB - 1:
+                for f in range(4, fields):
+                    keep(f)
             conds, freezes = [], []
             for i in range(steps):
                 t, qv, ql, qi = [cur[f][i] for f in range(4)]
@@ -309,41 +334,35 @@
                 conds.append(cond)
                 freezes.append(freeze)
             changes += conds + freezes
-        for f in range(fields):
-            for i in range(steps):
-                out_buf[half, f, pl.ds(i, SUBLANES, stride=steps), :] = cur[f][i]
-            new_ref[f, :, lanes] = out_buf[half, f].astype(BF16)
-        return jnp.concatenate(changes, axis=0)
+        for f in range(4):
+            keep(f)
+        for n, value in enumerate(changes):
+            change_ref[n * SUBLANES : (n + 1) * SUBLANES, half * LANES : (half + 1) * LANES] = value
 
     cells = pair_lanes // width
     group = iota((pair_lanes, LANES), 0) // width == iota((pair_lanes, LANES), 1) % cells
     total = jnp.where(group, 1.0, 0.0).astype(BF16)
 
-    def pair(p, carry):
-        load(p).wait()
-        mine = lane // cells == p
-        lanes = pl.ds(pl.multiple_of(p * pair_lanes, pair_lanes), pair_lanes)
-        for f in range(fields):
-            sums = dot_nn(state_ref[f, :, lanes], total, None)
-            keep = jnp.broadcast_to(mine[0:1, :], sums.shape)
-            base_ref[f] = jnp.where(keep, sums, base_ref[f])
-        change = jnp.concatenate([element(2 * p, 0), element(2 * p + 1, 1)], axis=1)
+    def set_sums(ref, p, sums):
+        mine = jnp.broadcast_to(lane[0:1, :] // cells == p, sums.shape)
+        ref[...] = jnp.where(mine, sums, ref[...])
+
+    def sum_changes(p):
+        change = change_ref[...]
         high = change.astype(BF16)
         low = (change - high.astype(F32)).astype(BF16)
-        sums = dot_nn(high, total, None) + dot_nn(low, total, None)
-        keep = jnp.broadcast_to(mine[0:1, :], sums.shape)
-        inc_ref[...] = jnp.where(keep, sums, inc_ref[...])
+        set_sums(inc_ref, p, dot_nn(high, total, None) + dot_nn(low, total, None))
+
+    def pair(p, carry):
+        sum_changes(p - 1)
+        widen(2 * p + 1, 1)
+        advance_element(2 * p, 0)
+        for f in range(fields):
+            set_sums(base_ref.at[f], p, dot_nn(state_ref[f, :, lanes_at(2 * p, 2)], total, None))
+        widen(jnp.minimum(2 * p + 2, size.elements - 1), 0)
+        advance_element(2 * p + 1, 1)
         return carry
 
-    lax.fori_loop(0, pairs, pair, 0)
-
-    def change_of(n):
-        return [
-            inc_ref[(n * steps + i) * SUBLANES : (n * steps + i + 1) * SUBLANES, :]
-            for i in range(steps)
-        ]
-
-    parts = [[change_of(2 * n), change_of(2 * n + 1)] for n in range(NSUB)]
     parity = lax.axis_index("tile") % 2
     slots_row = flat_row(params[6:10, 0 : size.elements])
     codes_row = flat_row(params[10:14, 0 : size.elements])
@@ -360,6 +379,19 @@
     picked = dot_nt(cell, select, None).astype(I32)
     source = jnp.where(lane < size.cells, lane, picked)
 
+    for f in range(fields):
+        load(f).wait()
+    widen(0, 0)
+    lax.fori_loop(0, pairs, pair, 0)
+    sum_changes(pairs - 1)
+
+    def change_of(n):
+        return [
+            inc_ref[(n * steps + i) * SUBLANES : (n * steps + i + 1) * SUBLANES, :]
+            for i in range(steps)
+        ]
+
+    parts = [[change_of(2 * n), change_of(2 * n + 1)] for n in range(NSUB)]
     scale = PER_TIME / width
     columns = []
     for f in range(fields):
@@ -426,7 +458,8 @@
 
 def message_kernel(size, own_ref, twin_ref, part_ref, even_ref, odd_ref):
     cells = jnp.concatenate([own_ref[0 : size.cells, :], twin_ref[0 : size.cells, :]], axis=0)
-    part = dot_nn(part_ref[:, 0 : 2 * size.cells], cells)
+    weights = stack_left(part_ref[:, 0 : 2 * size.cells], 1)
+    part = dot_nn(weights, stack_right(cells, 0), None)
     lane = iota((2 * size.part, size.wide), 1)
     part = jnp.where(lane == size.flat, part_ref[:, size.columns : size.columns + 1], part)
     part = jnp.where(lane == size.flat + 1, part_ref[:, size.ops : size.ops + 1], part)
@@ -528,7 +561,8 @@
     side = matrix_ref[2 * raw : n, :]
     mass_sum = matrix_ref[n : n + 1, :] + jnp.sum(side * mass, axis=0, keepdims=True)
     keep_ref[...] = jnp.broadcast_to(mass_sum, (8, size.points))
-    total = sum_ref[...] + dot_tn(rows[:, 0 : size.flat], matrix_ref[0:n, :])
+    wide = dot_tn(stack_left(rows, 0), stack_right(matrix_ref[0:n, :], 0), None)
+    total = sum_ref[...] + wide[0 : size.flat, :]
     total = total / mass_sum
     steps = levels // SUBLANES
     for f in range(size.flat // levels):
@@ -582,7 +616,8 @@
             block,
             pltpu.VMEM((fields, levels, LANES), F32),
             pltpu.VMEM((2 * NSUB * levels, LANES), F32),
-            pltpu.SemaphoreType.DMA((size.elements // 2,)),
+            pltpu.VMEM((2 * NSUB * levels, 2 * LANES), F32),
+            pltpu.SemaphoreType.DMA((fields,)),
             pltpu.SemaphoreType.DMA((len(params),)),
         ],
         limit=16,

time: 20.2 us -> 19.6 us (0.970)
  Pallas kernels: 8.08 us -> 7.54 us
    pallas_call x5, Pallas kernels: 8.08 us -> 7.54 us  [call(): pl.pallas_call(body, out_shape=outs, in_specs=in_specs or [VMEM] * len(in...]
where the time goes in v3:
time: 19.6 us; the launch traced here: 19.4 us
  starting transfers between devices  7.94 us (41%)
  Pallas kernels  7.54 us (38%)
  waiting for transfers between devices  2.51 us (13%)
  local copies, waits for them, and re-layouts  0.71 us (4%)
  between operations  0.69 us (4%)
    pallas_call x5, Pallas kernels, call(): pl.pallas_call(body, out_shape=outs, in_specs=in_specs or [VMEM] * len(in...  7.54 us
    ppermute x2, starting transfers between devices, swap(): return lax.ppermute(value, 'tile', swap_pairs(odd))  7.38 us
    ppermute x2, waiting for transfers between devices, swap(): return lax.ppermute(value, 'tile', swap_pairs(odd))  2.14 us
    unnamed x4, local copies, waits for them, and re-layouts  0.71 us
    ppermute x1, starting transfers between devices, shift(): lax.ppermute(value, axis, [(s, (s + steps) % count) for s in range(count)])  0.56 us
  transfers between devices with their start and end apart: 3, of which 2 were waited for; matrix products, arithmetic and copies ran while one was open for 0% of the time, Pallas kernels for 9%

profile of v3, /device:TPU:0, one launch (start us, length us, event | category | flops | bytes accessed | tf_op | source)
XLA Modules:
  0.0 19.4 jit_solution(6686308279464436919)
XLA Ops:
  0.6 0.0 copy-start
  0.6 5.3 %advance.1 = (bf16[6,72,1024]{2,1,0:T(8,128)(2,1)S(1)}, f32[56,512]{1,0:T(8,128)S(1)}) custom-call(bf16[6,72,1024]{2,1,0:T(8,128)(2,1)} %refs_0_.1, s32[1,32]{1,0:T(1,128)} %bitcast.31, f32[1,32]{1,0:T(1,128)} %bitcast.32, f32[1,32]{1,0:T(1,128)} %bitcast.33, f32[1,32]{1,0:T(1,128)} %bitcast.34, f32[1,72]{1,0:T(1,128)} %bitcast.35, f32[1,128]{1,0:T(1,128)} %bitcast.36, ...), custom_call_target="tpu_custom_call" | custom-call | tf_op jit(solution)/shard_map/advance/pallas_call | solution.py:580
  5.9 0.6 %collective-permute-start.2 = (f32[56,512]{1,0:T(8,128)S(1)}, f32[56,512]{1,0:T(8,128)S(1)}, u32[]{:S(2)}, u32[]{:S(2)}) collective-permute-start(f32[56,512]{1,0:T(8,128)S(1)} %get-tuple-element.81.own_ref), channel_id=1, source_target_pairs={{0,16},{16,0},{1,17},{17,1},{2,18},{18,2},{3,19},{19,3},{4,20},{20... | collective-permute-start | bytes 344072 | tf_op jit(solution)/shard_map/ppermute | solution.py:642
  6.5 0.0 copy-done
  6.5 0.6 %weights.1.part_ref = f32[32,128]{1,0:T(8,128)S(1)} custom-call(f32[56,512]{1,0:T(8,128)S(1)} %get-tuple-element.81.own_ref, f32[224,128]{1,0:T(8,128)S(1)} %copy-done), custom_call_target="tpu_custom_call" | custom-call | tf_op jit(solution)/shard_map/weights/pallas_call | solution.py:580
  7.1 0.4 %collective-permute-done.2.twin_ref = f32[56,512]{1,0:T(8,128)S(1)} collective-permute-done((f32[56,512]{1,0:T(8,128)S(1)}, f32[56,512]{1,0:T(8,128)S(1)}, u32[]{:S(2)}, u32[]{:S(2)}) %collective-permute-start.2) | collective-permute-done | bytes 114720 | tf_op jit(solution)/shard_map/ppermute | solution.py:642
  7.4 0.2 message.1
  7.6 2.9 %collective-permute-start.3 = (f32[32,512]{1,0:T(8,128)S(1)}, f32[32,512]{1,0:T(8,128)S(1)}, u32[]{:S(2)}, u32[]{:S(2)}) collective-permute-start(f32[32,512]{1,0:T(8,128)S(1)} %get-tuple-element.84), channel_id=1, source_target_pairs={{0,1},{1,0},{2,3},{3,2},{4,5},{5,4},{6,7},{7,6},{8,9},{9,8},{10,11... | collective-permute-start | bytes 196616 | tf_op jit(solution)/shard_map/ppermute | solution.py:637
  10.5 4.5 %collective-permute-start.4 = (f32[32,512]{1,0:T(8,128)S(1)}, f32[32,512]{1,0:T(8,128)S(1)}, u32[]{:S(2)}, u32[]{:S(2)}) collective-permute-start(f32[32,512]{1,0:T(8,128)S(1)} %get-tuple-element.85), channel_id=1, source_target_pairs={{0,15},{1,2},{2,1},{3,4},{4,3},{5,6},{6,5},{7,8},{8,7},{9,10},{10,... | collective-permute-start | bytes 196616 | tf_op jit(solution)/shard_map/ppermute | solution.py:637
  15.0 1.2 %inner.1 = (f32[432,128]{1,0:T(8,128)S(1)}, f32[32,512]{1,0:T(8,128)S(1)}, f32[72,128]{1,0:T(8,128)S(1)}, bf16[6,72,1024]{2,1,0:T(8,128)(2,1)}) custom-call(f32[224,128]{1,0:T(8,128)S(1)} %copy-done, f32[56,512]{1,0:T(8,128)S(1)} %get-tuple-element.81.own_ref, f32[56,512]{1,0:T(8,128)S(1)} %collective-permute-done.2.twin_ref, ...), custom_call_target="tpu_custom_call" | custom-call | tf_op jit(solution)/shard_map/inner/pallas_call | solution.py:580
  16.2 0.0 collective-permute-done.3.even_ref
  16.2 2.1 %collective-permute-done.4.odd_ref = f32[32,512]{1,0:T(8,128)S(1)} collective-permute-done((f32[32,512]{1,0:T(8,128)S(1)}, f32[32,512]{1,0:T(8,128)S(1)}, u32[]{:S(2)}, u32[]{:S(2)}) %collective-permute-start.4) | collective-permute-done | bytes 65568 | tf_op jit(solution)/shard_map/ppermute | solution.py:637
  18.3 0.3 %final.1 = (f32[432,128]{1,0:T(8,128)S(1)}, f32[8,128]{1,0:T(8,128)S(1)}, s32[1,1]{1,0:T(1,128)S(4)}) custom-call(f32[32,512]{1,0:T(8,128)S(1)} %collective-permute-done.3.even_ref, f32[32,512]{1,0:T(8,128)S(1)} %collective-permute-done.4.odd_ref, f32[432,128]{1,0:T(8,128)S(1)} %get-tuple-element.86.sum_ref, f32[32,512]{1,0:T(8,128)S(1)} %get-tuple-element.87.near_ref, ...), custom_call_target="tpu_custom_call" | custom-call | tf_op jit(solution)/shard_map/final/pallas_call | solution.py:580
  18.7 0.7 %copy.28 = f32[6,72,128]{2,1,0:T(8,128)} copy(f32[6,72,128]{2,1,0:T(8,128)S(1)} %get-tuple-element.102) | data formatting | bytes 442368
  (2 shorter events, 0.0 us)
Async XLA Ops:
  0.6 5.8 %copy-start = (f32[224,128]{1,0:T(8,128)S(1)}, f32[224,128]{1,0:T(8,128)}, u32[]{:S(2)}) copy-start(f32[224,128]{1,0:T(8,128)} %constant.6.clone.table_ref) | copy-start | bytes 344068
  5.9 1.5 %collective-permute-start.2 = (f32[56,512]{1,0:T(8,128)S(1)}, f32[56,512]{1,0:T(8,128)S(1)}, u32[]{:S(2)}, u32[]{:S(2)}) collective-permute-start(f32[56,512]{1,0:T(8,128)S(1)} %get-tuple-element.81.own_ref), channel_id=1, source_target_pairs={{0,16},{16,0},{1,17},{17,1},{2,18},{18,2},{3,19},{19,3},{4,20},{20... | collective-permute-start | bytes 344072 | tf_op jit(solution)/shard_map/ppermute | solution.py:642
  7.6 8.6 %collective-permute-start.3 = (f32[32,512]{1,0:T(8,128)S(1)}, f32[32,512]{1,0:T(8,128)S(1)}, u32[]{:S(2)}, u32[]{:S(2)}) collective-permute-start(f32[32,512]{1,0:T(8,128)S(1)} %get-tuple-element.84), channel_id=1, source_target_pairs={{0,1},{1,0},{2,3},{3,2},{4,5},{5,4},{6,7},{7,6},{8,9},{9,8},{10,11... | collective-permute-start | bytes 196616 | tf_op jit(solution)/shard_map/ppermute | solution.py:637
  10.5 7.9 %collective-permute-start.4 = (f32[32,512]{1,0:T(8,128)S(1)}, f32[32,512]{1,0:T(8,128)S(1)}, u32[]{:S(2)}, u32[]{:S(2)}) collective-permute-start(f32[32,512]{1,0:T(8,128)S(1)} %get-tuple-element.85), channel_id=1, source_target_pairs={{0,15},{1,2},{2,1},{3,4},{4,3},{5,6},{6,5},{7,8},{8,7},{9,10},{10,... | collective-permute-start | bytes 196616 | tf_op jit(solution)/shard_map/ppermute | solution.py:637

commit v4 on v3

--- a/solution.py
+++ b/solution.py
@@ -285,27 +285,31 @@
     def lanes_at(e, count=1):
         return pl.ds(pl.multiple_of(e * LANES, LANES), count * LANES)
 
-    def widen(e, half):
+    def column_rows(e):
+        here = lanes_of(params[0:SUBLANES, :], e * per_lane + lane // width)
+        active, mix, drift, rate = [
+            jnp.broadcast_to(here[r : r + 1, :], full) for r in range(4)
+        ]
+        return active, rate, (1.0 - 2.0 * mix, mix - 0.5 * drift, mix + 0.5 * drift)
+
+    def transport(value, weights):
+        centre, east_c, west_c = weights
+        east, west = lanes_of(value, east_lane), lanes_of(value, west_lane)
+        return centre * value + east_c * east + west_c * west
+
+    def transport_first(e, half):
+        _, _, weights = column_rows(e)
         for f in range(fields):
-            wide_ref[half, f] = state_ref[f, :, lanes_at(e)].astype(F32)
+            value = state_ref[f, :, lanes_at(e)].astype(F32)
+            for i in range(steps):
+                rows = slice(i * SUBLANES, (i + 1) * SUBLANES)
+                wide_ref[half, f, rows, :] = transport(value[rows, :], weights)
 
     def advance_element(e, half):
-        here = lanes_of(params[0:SUBLANES, :], e * per_lane + lane // width)
-
-        def row(r):
-            return jnp.broadcast_to(here[r : r + 1, :], full)
-
-        active, mix, drift, rate = row(0).astype(I32), row(1), row(2), row(3)
-        centre, east_c, west_c = 1.0 - 2.0 * mix, mix - 0.5 * drift, mix + 0.5 * drift
+        active, rate, weights = column_rows(e)
+        active = active.astype(I32)
         alive = [v < active for v in level]
         ice = [jnp.where(v, 0.15, 0.0) for v in alive]
-
-        def transport(a):
-            a = [
-                centre * v + east_c * lanes_of(v, east_lane) + west_c * lanes_of(v, west_lane)
-                for v in a
-            ]
-            return vertical(a)
 
         def keep(f):
             for i in range(steps):
@@ -315,7 +319,9 @@
         cur = [[spread(wide_ref.at[half, f], i) for i in range(steps)] for f in range(fields)]
         changes = []
         for substep in range(NSUB):
-            cur = [transport(a) for a in cur]
+            if substep > 0:
+                cur = [[transport(v, weights) for v in a] for a in cur]
+            cur = [vertical(a) for a in cur]
             if substep == NSUB - 1:
                 for f in range(4, fields):
                     keep(f)
@@ -355,14 +361,27 @@
 
     def pair(p, carry):
         sum_changes(p - 1)
-        widen(2 * p + 1, 1)
+        transport_first(2 * p + 1, 1)
         advance_element(2 * p, 0)
         for f in range(fields):
             set_sums(base_ref.at[f], p, dot_nn(state_ref[f, :, lanes_at(2 * p, 2)], total, None))
-        widen(jnp.minimum(2 * p + 2, size.elements - 1), 0)
+        transport_first(jnp.minimum(2 * p + 2, size.elements - 1), 0)
         advance_element(2 * p + 1, 1)
         return carry
 
+    for f in range(fields):
+        load(f).wait()
+    transport_first(0, 0)
+    lax.fori_loop(0, pairs, pair, 0)
+    sum_changes(pairs - 1)
+
+    def change_of(n):
+        return [
+            inc_ref[(n * steps + i) * SUBLANES : (n * steps + i + 1) * SUBLANES, :]
+            for i in range(steps)
+        ]
+
+    parts = [[change_of(2 * n), change_of(2 * n + 1)] for n in range(NSUB)]
     parity = lax.axis_index("tile") % 2
     slots_row = flat_row(params[6:10, 0 : size.elements])
     codes_row = flat_row(params[10:14, 0 : size.elements])
@@ -379,19 +398,6 @@
     picked = dot_nt(cell, select, None).astype(I32)
     source = jnp.where(lane < size.cells, lane, picked)
 
-    for f in range(fields):
-        load(f).wait()
-    widen(0, 0)
-    lax.fori_loop(0, pairs, pair, 0)
-    sum_changes(pairs - 1)
-
-    def change_of(n):
-        return [
-            inc_ref[(n * steps + i) * SUBLANES : (n * steps + i + 1) * SUBLANES, :]
-            for i in range(steps)
-        ]
-
-    parts = [[change_of(2 * n), change_of(2 * n + 1)] for n in range(NSUB)]
     scale = PER_TIME / width
     columns = []
     for f in range(fields):

time: 19.6 us -> 19.3 us (0.985)
  Pallas kernels: 7.54 us -> 7.29 us
    pallas_call x5, Pallas kernels: 7.54 us -> 7.29 us  [call(): pl.pallas_call(body, out_shape=outs, in_specs=in_specs or [VMEM] * len(in...]
where the time goes in v4:
time: 19.3 us; the launch traced here: 19.2 us
  starting transfers between devices  7.94 us (41%)
  Pallas kernels  7.29 us (38%)
  waiting for transfers between devices  2.51 us (13%)
  local copies, waits for them, and re-layouts  0.71 us (4%)
  between operations  0.69 us (4%)
    ppermute x2, starting transfers between devices, swap(): return lax.ppermute(value, 'tile', swap_pairs(odd))  7.38 us
    pallas_call x5, Pallas kernels, call(): pl.pallas_call(body, out_shape=outs, in_specs=in_specs or [VMEM] * len(in...  7.29 us
    ppermute x2, waiting for transfers between devices, swap(): return lax.ppermute(value, 'tile', swap_pairs(odd))  2.14 us
    unnamed x4, local copies, waits for them, and re-layouts  0.71 us
    ppermute x1, starting transfers between devices, shift(): lax.ppermute(value, axis, [(s, (s + steps) % count) for s in range(count)])  0.56 us
  transfers between devices with their start and end apart: 3, of which 2 were waited for; matrix products, arithmetic and copies ran while one was open for 0% of the time, Pallas kernels for 9%

profile of v4, /device:TPU:0, one launch (start us, length us, event | category | flops | bytes accessed | tf_op | source)
XLA Modules:
  0.0 19.2 jit_solution(5473718509582541367)
XLA Ops:
  0.6 0.0 copy-start
  0.6 5.0 %advance.1 = (bf16[6,72,1024]{2,1,0:T(8,128)(2,1)S(1)}, f32[56,512]{1,0:T(8,128)S(1)}) custom-call(bf16[6,72,1024]{2,1,0:T(8,128)(2,1)} %refs_0_.1, s32[1,32]{1,0:T(1,128)} %bitcast.31, f32[1,32]{1,0:T(1,128)} %bitcast.32, f32[1,32]{1,0:T(1,128)} %bitcast.33, f32[1,32]{1,0:T(1,128)} %bitcast.34, f32[1,72]{1,0:T(1,128)} %bitcast.35, f32[1,128]{1,0:T(1,128)} %bitcast.36, ...), custom_call_target="tpu_custom_call" | custom-call | tf_op jit(solution)/shard_map/advance/pallas_call | solution.py:586
  5.7 0.6 %collective-permute-start.2 = (f32[56,512]{1,0:T(8,128)S(1)}, f32[56,512]{1,0:T(8,128)S(1)}, u32[]{:S(2)}, u32[]{:S(2)}) collective-permute-start(f32[56,512]{1,0:T(8,128)S(1)} %get-tuple-element.81.own_ref), channel_id=1, source_target_pairs={{0,16},{16,0},{1,17},{17,1},{2,18},{18,2},{3,19},{19,3},{4,20},{20... | collective-permute-start | bytes 344072 | tf_op jit(solution)/shard_map/ppermute | solution.py:648
  6.2 0.0 copy-done
  6.2 0.6 %weights.1.part_ref = f32[32,128]{1,0:T(8,128)S(1)} custom-call(f32[56,512]{1,0:T(8,128)S(1)} %get-tuple-element.81.own_ref, f32[224,128]{1,0:T(8,128)S(1)} %copy-done), custom_call_target="tpu_custom_call" | custom-call | tf_op jit(solution)/shard_map/weights/pallas_call | solution.py:586
  6.8 0.4 %collective-permute-done.2.twin_ref = f32[56,512]{1,0:T(8,128)S(1)} collective-permute-done((f32[56,512]{1,0:T(8,128)S(1)}, f32[56,512]{1,0:T(8,128)S(1)}, u32[]{:S(2)}, u32[]{:S(2)}) %collective-permute-start.2) | collective-permute-done | bytes 114720 | tf_op jit(solution)/shard_map/ppermute | solution.py:648
  7.2 0.2 message.1
  7.4 2.9 %collective-permute-start.3 = (f32[32,512]{1,0:T(8,128)S(1)}, f32[32,512]{1,0:T(8,128)S(1)}, u32[]{:S(2)}, u32[]{:S(2)}) collective-permute-start(f32[32,512]{1,0:T(8,128)S(1)} %get-tuple-element.84), channel_id=1, source_target_pairs={{0,1},{1,0},{2,3},{3,2},{4,5},{5,4},{6,7},{7,6},{8,9},{9,8},{10,11... | collective-permute-start | bytes 196616 | tf_op jit(solution)/shard_map/ppermute | solution.py:643
  10.2 4.5 %collective-permute-start.4 = (f32[32,512]{1,0:T(8,128)S(1)}, f32[32,512]{1,0:T(8,128)S(1)}, u32[]{:S(2)}, u32[]{:S(2)}) collective-permute-start(f32[32,512]{1,0:T(8,128)S(1)} %get-tuple-element.85), channel_id=1, source_target_pairs={{0,15},{1,2},{2,1},{3,4},{4,3},{5,6},{6,5},{7,8},{8,7},{9,10},{10,... | collective-permute-start | bytes 196616 | tf_op jit(solution)/shard_map/ppermute | solution.py:643
  14.7 1.2 %inner.1 = (f32[432,128]{1,0:T(8,128)S(1)}, f32[32,512]{1,0:T(8,128)S(1)}, f32[72,128]{1,0:T(8,128)S(1)}, bf16[6,72,1024]{2,1,0:T(8,128)(2,1)}) custom-call(f32[224,128]{1,0:T(8,128)S(1)} %copy-done, f32[56,512]{1,0:T(8,128)S(1)} %get-tuple-element.81.own_ref, f32[56,512]{1,0:T(8,128)S(1)} %collective-permute-done.2.twin_ref, ...), custom_call_target="tpu_custom_call" | custom-call | tf_op jit(solution)/shard_map/inner/pallas_call | solution.py:586
  15.9 0.0 collective-permute-done.3.even_ref
  15.9 2.1 %collective-permute-done.4.odd_ref = f32[32,512]{1,0:T(8,128)S(1)} collective-permute-done((f32[32,512]{1,0:T(8,128)S(1)}, f32[32,512]{1,0:T(8,128)S(1)}, u32[]{:S(2)}, u32[]{:S(2)}) %collective-permute-start.4) | collective-permute-done | bytes 65568 | tf_op jit(solution)/shard_map/ppermute | solution.py:643
  18.1 0.3 %final.1 = (f32[432,128]{1,0:T(8,128)S(1)}, f32[8,128]{1,0:T(8,128)S(1)}, s32[1,1]{1,0:T(1,128)S(4)}) custom-call(f32[32,512]{1,0:T(8,128)S(1)} %collective-permute-done.3.even_ref, f32[32,512]{1,0:T(8,128)S(1)} %collective-permute-done.4.odd_ref, f32[432,128]{1,0:T(8,128)S(1)} %get-tuple-element.86.sum_ref, f32[32,512]{1,0:T(8,128)S(1)} %get-tuple-element.87.near_ref, ...), custom_call_target="tpu_custom_call" | custom-call | tf_op jit(solution)/shard_map/final/pallas_call | solution.py:586
  18.5 0.7 %copy.28 = f32[6,72,128]{2,1,0:T(8,128)} copy(f32[6,72,128]{2,1,0:T(8,128)S(1)} %get-tuple-element.102) | data formatting | bytes 442368
  (2 shorter events, 0.0 us)
Async XLA Ops:
  0.6 5.6 %copy-start = (f32[224,128]{1,0:T(8,128)S(1)}, f32[224,128]{1,0:T(8,128)}, u32[]{:S(2)}) copy-start(f32[224,128]{1,0:T(8,128)} %constant.6.clone.table_ref) | copy-start | bytes 344068
  5.7 1.5 %collective-permute-start.2 = (f32[56,512]{1,0:T(8,128)S(1)}, f32[56,512]{1,0:T(8,128)S(1)}, u32[]{:S(2)}, u32[]{:S(2)}) collective-permute-start(f32[56,512]{1,0:T(8,128)S(1)} %get-tuple-element.81.own_ref), channel_id=1, source_target_pairs={{0,16},{16,0},{1,17},{17,1},{2,18},{18,2},{3,19},{19,3},{4,20},{20... | collective-permute-start | bytes 344072 | tf_op jit(solution)/shard_map/ppermute | solution.py:648
  7.4 8.6 %collective-permute-start.3 = (f32[32,512]{1,0:T(8,128)S(1)}, f32[32,512]{1,0:T(8,128)S(1)}, u32[]{:S(2)}, u32[]{:S(2)}) collective-permute-start(f32[32,512]{1,0:T(8,128)S(1)} %get-tuple-element.84), channel_id=1, source_target_pairs={{0,1},{1,0},{2,3},{3,2},{4,5},{5,4},{6,7},{7,6},{8,9},{9,8},{10,11... | collective-permute-start | bytes 196616 | tf_op jit(solution)/shard_map/ppermute | solution.py:643
  10.2 7.9 %collective-permute-start.4 = (f32[32,512]{1,0:T(8,128)S(1)}, f32[32,512]{1,0:T(8,128)S(1)}, u32[]{:S(2)}, u32[]{:S(2)}) collective-permute-start(f32[32,512]{1,0:T(8,128)S(1)} %get-tuple-element.85), channel_id=1, source_target_pairs={{0,15},{1,2},{2,1},{3,4},{4,3},{5,6},{6,5},{7,8},{8,7},{9,10},{10,... | collective-permute-start | bytes 196616 | tf_op jit(solution)/shard_map/ppermute | solution.py:643

commit v5 on v4

--- a/solution.py
+++ b/solution.py
@@ -246,9 +246,6 @@
     for f in range(fields):
         load(f).start()
     table_ref[...] = jnp.zeros(table_ref.shape, F32)
-    change_ref[...] = jnp.zeros(change_ref.shape, F32)
-    base_ref[...] = jnp.zeros(base_ref.shape, F32)
-    inc_ref[...] = jnp.zeros(inc_ref.shape, F32)
     for copy in small:
         copy.wait()
     first = 0

time: 19.3 us -> 19.3 us (level)
  no operation moved by 1% of the time
where the time goes in v5:
time: 19.3 us; the launch traced here: 19.2 us
  starting transfers between devices  7.94 us (41%)
  Pallas kernels  7.29 us (38%)
  waiting for transfers between devices  2.51 us (13%)
  local copies, waits for them, and re-layouts  0.71 us (4%)
  between operations  0.69 us (4%)
    ppermute x2, starting transfers between devices, swap(): return lax.ppermute(value, 'tile', swap_pairs(odd))  7.38 us
    pallas_call x5, Pallas kernels, call(): pl.pallas_call(body, out_shape=outs, in_specs=in_specs or [VMEM] * len(in...  7.29 us
    ppermute x2, waiting for transfers between devices, swap(): return lax.ppermute(value, 'tile', swap_pairs(odd))  2.14 us
    unnamed x4, local copies, waits for them, and re-layouts  0.71 us
    ppermute x1, starting transfers between devices, shift(): lax.ppermute(value, axis, [(s, (s + steps) % count) for s in range(count)])  0.56 us
  transfers between devices with their start and end apart: 3, of which 2 were waited for; matrix products, arithmetic and copies ran while one was open for 0% of the time, Pallas kernels for 9%

profile of v5, /device:TPU:0, one launch (start us, length us, event | category | flops | bytes accessed | tf_op | source)
XLA Modules:
  0.0 19.2 jit_solution(7506671258107176051)
XLA Ops:
  0.6 0.0 copy-start
  0.6 5.0 %advance.1 = (bf16[6,72,1024]{2,1,0:T(8,128)(2,1)S(1)}, f32[56,512]{1,0:T(8,128)S(1)}) custom-call(bf16[6,72,1024]{2,1,0:T(8,128)(2,1)} %refs_0_.1, s32[1,32]{1,0:T(1,128)} %bitcast.31, f32[1,32]{1,0:T(1,128)} %bitcast.32, f32[1,32]{1,0:T(1,128)} %bitcast.33, f32[1,32]{1,0:T(1,128)} %bitcast.34, f32[1,72]{1,0:T(1,128)} %bitcast.35, f32[1,128]{1,0:T(1,128)} %bitcast.36, ...), custom_call_target="tpu_custom_call" | custom-call | tf_op jit(solution)/shard_map/advance/pallas_call | solution.py:583
  5.7 0.6 %collective-permute-start.2 = (f32[56,512]{1,0:T(8,128)S(1)}, f32[56,512]{1,0:T(8,128)S(1)}, u32[]{:S(2)}, u32[]{:S(2)}) collective-permute-start(f32[56,512]{1,0:T(8,128)S(1)} %get-tuple-element.81.own_ref), channel_id=1, source_target_pairs={{0,16},{16,0},{1,17},{17,1},{2,18},{18,2},{3,19},{19,3},{4,20},{20... | collective-permute-start | bytes 344072 | tf_op jit(solution)/shard_map/ppermute | solution.py:645
  6.2 0.0 copy-done
  6.2 0.6 %weights.1.part_ref = f32[32,128]{1,0:T(8,128)S(1)} custom-call(f32[56,512]{1,0:T(8,128)S(1)} %get-tuple-element.81.own_ref, f32[224,128]{1,0:T(8,128)S(1)} %copy-done), custom_call_target="tpu_custom_call" | custom-call | tf_op jit(solution)/shard_map/weights/pallas_call | solution.py:583
  6.8 0.4 %collective-permute-done.2.twin_ref = f32[56,512]{1,0:T(8,128)S(1)} collective-permute-done((f32[56,512]{1,0:T(8,128)S(1)}, f32[56,512]{1,0:T(8,128)S(1)}, u32[]{:S(2)}, u32[]{:S(2)}) %collective-permute-start.2) | collective-permute-done | bytes 114720 | tf_op jit(solution)/shard_map/ppermute | solution.py:645
  7.2 0.2 message.1
  7.4 2.9 %collective-permute-start.3 = (f32[32,512]{1,0:T(8,128)S(1)}, f32[32,512]{1,0:T(8,128)S(1)}, u32[]{:S(2)}, u32[]{:S(2)}) collective-permute-start(f32[32,512]{1,0:T(8,128)S(1)} %get-tuple-element.84), channel_id=1, source_target_pairs={{0,1},{1,0},{2,3},{3,2},{4,5},{5,4},{6,7},{7,6},{8,9},{9,8},{10,11... | collective-permute-start | bytes 196616 | tf_op jit(solution)/shard_map/ppermute | solution.py:640
  10.2 4.5 %collective-permute-start.4 = (f32[32,512]{1,0:T(8,128)S(1)}, f32[32,512]{1,0:T(8,128)S(1)}, u32[]{:S(2)}, u32[]{:S(2)}) collective-permute-start(f32[32,512]{1,0:T(8,128)S(1)} %get-tuple-element.85), channel_id=1, source_target_pairs={{0,15},{1,2},{2,1},{3,4},{4,3},{5,6},{6,5},{7,8},{8,7},{9,10},{10,... | collective-permute-start | bytes 196616 | tf_op jit(solution)/shard_map/ppermute | solution.py:640
  14.7 1.2 %inner.1 = (f32[432,128]{1,0:T(8,128)S(1)}, f32[32,512]{1,0:T(8,128)S(1)}, f32[72,128]{1,0:T(8,128)S(1)}, bf16[6,72,1024]{2,1,0:T(8,128)(2,1)}) custom-call(f32[224,128]{1,0:T(8,128)S(1)} %copy-done, f32[56,512]{1,0:T(8,128)S(1)} %get-tuple-element.81.own_ref, f32[56,512]{1,0:T(8,128)S(1)} %collective-permute-done.2.twin_ref, ...), custom_call_target="tpu_custom_call" | custom-call | tf_op jit(solution)/shard_map/inner/pallas_call | solution.py:583
  15.9 0.0 collective-permute-done.3.even_ref
  15.9 2.1 %collective-permute-done.4.odd_ref = f32[32,512]{1,0:T(8,128)S(1)} collective-permute-done((f32[32,512]{1,0:T(8,128)S(1)}, f32[32,512]{1,0:T(8,128)S(1)}, u32[]{:S(2)}, u32[]{:S(2)}) %collective-permute-start.4) | collective-permute-done | bytes 65568 | tf_op jit(solution)/shard_map/ppermute | solution.py:640
  18.1 0.3 %final.1 = (f32[432,128]{1,0:T(8,128)S(1)}, f32[8,128]{1,0:T(8,128)S(1)}, s32[1,1]{1,0:T(1,128)S(4)}) custom-call(f32[32,512]{1,0:T(8,128)S(1)} %collective-permute-done.3.even_ref, f32[32,512]{1,0:T(8,128)S(1)} %collective-permute-done.4.odd_ref, f32[432,128]{1,0:T(8,128)S(1)} %get-tuple-element.86.sum_ref, f32[32,512]{1,0:T(8,128)S(1)} %get-tuple-element.87.near_ref, ...), custom_call_target="tpu_custom_call" | custom-call | tf_op jit(solution)/shard_map/final/pallas_call | solution.py:583
  18.5 0.7 %copy.28 = f32[6,72,128]{2,1,0:T(8,128)} copy(f32[6,72,128]{2,1,0:T(8,128)S(1)} %get-tuple-element.102) | data formatting | bytes 442368
  (2 shorter events, 0.0 us)
Async XLA Ops:
  0.6 5.6 %copy-start = (f32[224,128]{1,0:T(8,128)S(1)}, f32[224,128]{1,0:T(8,128)}, u32[]{:S(2)}) copy-start(f32[224,128]{1,0:T(8,128)} %constant.6.clone.table_ref) | copy-start | bytes 344068
  5.7 1.5 %collective-permute-start.2 = (f32[56,512]{1,0:T(8,128)S(1)}, f32[56,512]{1,0:T(8,128)S(1)}, u32[]{:S(2)}, u32[]{:S(2)}) collective-permute-start(f32[56,512]{1,0:T(8,128)S(1)} %get-tuple-element.81.own_ref), channel_id=1, source_target_pairs={{0,16},{16,0},{1,17},{17,1},{2,18},{18,2},{3,19},{19,3},{4,20},{20... | collective-permute-start | bytes 344072 | tf_op jit(solution)/shard_map/ppermute | solution.py:645
  7.4 8.6 %collective-permute-start.3 = (f32[32,512]{1,0:T(8,128)S(1)}, f32[32,512]{1,0:T(8,128)S(1)}, u32[]{:S(2)}, u32[]{:S(2)}) collective-permute-start(f32[32,512]{1,0:T(8,128)S(1)} %get-tuple-element.84), channel_id=1, source_target_pairs={{0,1},{1,0},{2,3},{3,2},{4,5},{5,4},{6,7},{7,6},{8,9},{9,8},{10,11... | collective-permute-start | bytes 196616 | tf_op jit(solution)/shard_map/ppermute | solution.py:640
  10.2 7.9 %collective-permute-start.4 = (f32[32,512]{1,0:T(8,128)S(1)}, f32[32,512]{1,0:T(8,128)S(1)}, u32[]{:S(2)}, u32[]{:S(2)}) collective-permute-start(f32[32,512]{1,0:T(8,128)S(1)} %get-tuple-element.85), channel_id=1, source_target_pairs={{0,15},{1,2},{2,1},{3,4},{4,3},{5,6},{6,5},{7,8},{8,7},{9,10},{10,... | collective-permute-start | bytes 196616 | tf_op jit(solution)/shard_map/ppermute | solution.py:640
